TPU v7x, 32 devices: a whole 2x2x4 slice. The times are simulated.
32 devices in a mesh: dp: 4 (over y, core), seq: 8 (over z, x).
Axes of the slice: x: 2, y: 2, z: 4, core: 2. Of those that a mesh axis runs over, the one named last changes fastest.
Arguments:
- tokens: bfloat16 [32768, 2048], P(('dp', 'seq')), parts along dimension 0, may hold values from -6 to 6
- chosen: int32 [4096], P('dp'), parts along dimension 0, may hold values from 0 to 8191, as said below
- gates: float32 [4096], P('dp'), parts along dimension 0, may hold values from 0.5 to 2
- w_query: bfloat16 [2048, 1024], P('seq'), may hold values from -1.8561553 to 1.8561553
- w_key: bfloat16 [2048, 256], P('seq'), may hold values from -0.088388348 to 0.088388348
- w_value: bfloat16 [2048, 256], P('seq'), may hold values from -0.125 to 0.125
- w_out: bfloat16 [1024, 2048], P(None, 'seq'), may hold values from -0.5 to 0.5
Outputs:
- mixed: bfloat16 [32768, 2048], P(('dp', 'seq')), parts along dimension 0
There are 4 independent parts, one for each index of `dp`. A program takes and returns all parts, laid end to end along the dimension named above; an argument that names none is the same for every part. Nothing has to cross between parts.
Inputs may be any that keep to these rules, and one draw needn't show every extreme that they name: `chosen`: distinct positions in increasing order; at most 256 of them lie in one device's 1024 consecutive positions, and exactly 256 lie in some device's positions.
All inputs are finite; a program needn't handle non-finite values.
Results may differ from a plain program's by a relative error of at most 0.006.
Values may be sent and summed in bfloat16 or wider, within the bound.
A program may use at most 128 MiB of HBM per device.

v0:
```python
import functools

import jax
import jax.numpy as jnp
from jax import lax
from jax.experimental import pallas as pl
from jax.experimental.pallas import tpu as pltpu
from jax.sharding import PartitionSpec as P

HEADS = 8
KV_HEADS = 2
HEAD_DIM = 128
MOST_OWN = 256
MESH = pl.DeviceIdType.MESH
NEG = -1e30
F32 = jnp.float32
BF16 = jnp.bfloat16


class Ring:
    def __init__(self, geo, sems, region_in, region_y=None):
        self.g = geo
        self.sems = sems
        self.region_in = region_in
        self.region_y = region_y
        self.sends = []
        a_count, b_count = geo["A"], geo["B"]
        self.order = [(k, 0) for k in range(1, a_count)]
        self.order += [(k, j) for k in range(a_count) for j in range(1, b_count)]

    def piece(self, k, j):
        g = self.g
        a = lax.rem(g["a"] - k + g["A"], g["A"])
        b = lax.rem(g["b"] - j + g["B"], g["B"])
        return a * g["B"] + b

    def copy(self, kind, index, ref, dp, seq):
        send, recv = self.sems[kind]
        return pltpu.make_async_remote_copy(
            src_ref=ref,
            dst_ref=ref,
            send_sem=send.at[index],
            recv_sem=recv.at[index],
            device_id=(dp, seq),
            device_id_type=MESH,
        )

    def send(self, *args):
        made = self.copy(*args)
        made.start()
        self.sends.append(made)

    def arrive(self, kind, index, ref):
        self.copy(kind, index, ref, self.g["dp"], self.g["z_next"]).wait_recv()

    def mine(self, s):
        return self.region_in(s, self.g["y"], self.g["c"])

    def fan(self, k, j):
        if self.region_y is None:
            return
        g = self.g
        index = self.order.index((k, j))
        s = self.piece(k, j)
        self.send("y", index, self.region_y(s, g["y"], g["c"]), g["dp_y"], g["seq"])
        self.send("d", index, self.mine(s), g["dp_c"], g["seq"])

    def slow(self, k):
        g = self.g
        s = self.piece(k, 0)
        if k > 0:
            self.arrive("z", k - 1, self.mine(s))
        if k < g["A"] - 1:
            self.send("z", k, self.mine(s), g["dp"], g["z_next"])
        if g["B"] > 1:
            self.send("x", k * (g["B"] - 1), self.mine(s), g["dp"], g["x_next"])
        if k > 0:
            self.fan(k, 0)

    def fast(self, k, j):
        g = self.g
        s = self.piece(k, j)
        self.arrive("x", k * (g["B"] - 1) + j - 1, self.mine(s))
        if j < g["B"] - 1:
            self.send("x", k * (g["B"] - 1) + j, self.mine(s), g["dp"], g["x_next"])
        self.fan(k, j)

    def relay(self):
        g = self.g
        for index, (k, j) in enumerate(self.order):
            ref = self.region_y(self.piece(k, j), 1 - g["y"], g["c"])
            self.arrive("y", index, ref)
            self.send("d", len(self.order) + index, ref, g["dp_c"], g["seq"])

    def gather_core(self):
        g = self.g
        for index, (k, j) in enumerate(self.order):
            s = self.piece(k, j)
            self.arrive("d", index, self.region_in(s, g["y"], 1 - g["c"]))
            self.arrive("d", len(self.order) + index, self.region_y(s, 1 - g["y"], 1 - g["c"]))

    def finish(self):
        for made in self.sends:
            made.wait_send()


def main_kernel(
    A, B, tok, ch, wq, wk, wv, wo, blk, oh_out,
    tok_v, wbuf, obuf, kvbuf, normed, qs, acc, m_s, l_s, att, lsem,
    wz, wx, wy, wd, oz, ox, oy, od, kz, kx,
):
    n = A * B
    dp = lax.axis_index("dp")
    seq = lax.axis_index("seq")
    a, b = seq // B, lax.rem(seq, B)
    y, c = lax.rem(dp // 2, 2), lax.rem(dp, 2)
    z_next = lax.rem(a + 1, A) * B + b
    z_prev = lax.rem(a + A - 1, A) * B + b
    x_next = a * B + lax.rem(b + 1, B)
    x_prev = a * B + lax.rem(b + B - 1, B)
    dp_y = dp + 2 * (1 - 2 * y)
    dp_c = dp + 1 - 2 * c
    geo = dict(
        A=A, B=B, a=a, b=b, y=y, c=c, dp=dp, seq=seq,
        z_next=z_next, x_next=x_next, dp_y=dp_y, dp_c=dp_c,
    )
    t_rows = tok.shape[0]
    width = tok.shape[1]
    k_rows = wq.shape[0]
    q_cols, e_cols = wq.shape[1], wk.shape[1]
    all_cols = q_cols + 2 * e_cols
    o_rows, o_cols = wo.shape

    rows_here = pl.ds(pl.multiple_of(seq * k_rows, k_rows), k_rows)
    local = [
        (wq, wbuf.at[rows_here, pl.ds(0, q_cols)]),
        (wk, wbuf.at[rows_here, pl.ds(q_cols, e_cols)]),
        (wv, wbuf.at[rows_here, pl.ds(q_cols + e_cols, e_cols)]),
        (wo, obuf.at[seq]),
        (tok, tok_v),
    ]
    local = [pltpu.make_async_copy(s, d, lsem.at[i]) for i, (s, d) in enumerate(local)]
    for made in local:
        made.start()

    greet = [(dp, z_next)] + ([(dp, z_prev)] if A > 2 else [])
    if B > 1:
        greet += [(dp, x_next)] + ([(dp, x_prev)] if B > 2 else [])
    greet += [(dp_y, seq), (dp_c, seq)]
    barrier = pltpu.get_barrier_semaphore()
    for who in greet:
        pl.semaphore_signal(barrier, inc=1, device_id=who, device_id_type=MESH)
    pl.semaphore_wait(barrier, len(greet))

    third = all_cols // 6

    def w_region(s, start, size):
        return wbuf.at[
            pl.ds(pl.multiple_of(s * k_rows, k_rows), k_rows),
            pl.ds(pl.multiple_of(start, 128), size),
        ]

    o_half = o_rows // 2
    o_y = o_half * 3 // 8 // 16 * 16
    o_in = o_half - o_y

    def o_region(s, start, size):
        return obuf.at[s, pl.ds(pl.multiple_of(start, 16), size), :]

    ring_w = Ring(
        geo,
        {"z": wz, "x": wx, "y": wy, "d": wd},
        lambda s, y, c: w_region(s, c * (3 * third) + y * third, 2 * third),
        lambda s, y, c: w_region(s, c * (3 * third) + y * (2 * third), third),
    )
    ring_o = Ring(
        geo,
        {"z": oz, "x": ox, "y": oy, "d": od},
        lambda s, y, c: o_region(s, c * o_half + y * o_y, o_in),
        lambda s, y, c: o_region(s, c * o_half + y * o_in, o_y),
    )
    ring_k = Ring(geo, {"z": kz, "x": kx}, lambda s, y, c: kvbuf.at[s])

    for made in local[:3]:
        made.wait()
    ring_w.slow(0)

    base = seq * t_rows
    picks = ch[...]
    start = jnp.sum((picks < base).astype(F32), axis=1, keepdims=True)
    rel = picks - base
    inside = (rel >= 0) & (rel < t_rows)
    place = jnp.where(inside, (rel + 1).astype(F32), 0.0)
    order = lax.broadcasted_iota(jnp.int32, picks.shape, 1).astype(F32) - start
    slots = lax.broadcasted_iota(jnp.int32, (MOST_OWN, 1), 0).astype(F32)
    own = jnp.sum(jnp.where(order == slots, place, 0.0), axis=1, keepdims=True) - 1.0
    spots = lax.broadcasted_iota(jnp.int32, (1, t_rows), 1).astype(F32)
    oh_out[...] = (own == spots).astype(F32).astype(BF16)
    local[4].wait()
    chunk = 512
    square = jnp.zeros((MOST_OWN, 1), F32)
    for i in range(width // chunk):
        rows = jnp.dot(oh_out[...], tok_v[:, i * chunk : (i + 1) * chunk], preferred_element_type=F32)
        square = square + jnp.sum(rows * rows, axis=1, keepdims=True)
        normed[:, i * chunk : (i + 1) * chunk] = rows.astype(BF16)
    scale = lax.rsqrt(square / width + 1e-06)
    for i in range(width // chunk):
        cols = slice(i * chunk, (i + 1) * chunk)
        normed[:, cols] = (normed[:, cols].astype(F32) * scale).astype(BF16)

    for k in range(1, A):
        ring_w.slow(k)
        for j in range(1, B):
            ring_w.fast(k - 1, j)
    for j in range(1, B):
        ring_w.fast(A - 1, j)
    local[3].wait()
    ring_o.slow(0)
    ring_w.relay()
    ring_w.gather_core()

    kv_cols = 2 * e_cols
    for i in range(kv_cols // 256):
        part = jnp.dot(
            normed[...], wbuf[:, q_cols + i * 256 : q_cols + (i + 1) * 256], preferred_element_type=F32
        )
        kvbuf[seq, :, i * 256 : (i + 1) * 256] = part.astype(BF16)
    ring_k.slow(0)
    group = HEADS // KV_HEADS
    for i in range(q_cols // 256):
        part = jnp.dot(normed[...], wbuf[:, i * 256 : (i + 1) * 256], preferred_element_type=F32)
        part = (part * HEAD_DIM**-0.5).astype(BF16)
        for h in range(2):
            head = i * 2 + h
            first = (head % group) * MOST_OWN
            qs[head // group, first : first + MOST_OWN, :] = part[:, h * 128 : (h + 1) * 128]

    m_s[...] = jnp.full(m_s.shape, NEG, F32)
    l_s[...] = jnp.zeros(l_s.shape, F32)
    acc[...] = jnp.zeros(acc.shape, F32)

    def attend(t, diagonal):
        low = t * t_rows
        count = jnp.sum(
            ((picks >= low) & (picks < low + t_rows)).astype(F32), axis=1, keepdims=True
        )
        col = lax.broadcasted_iota(jnp.int32, (1, MOST_OWN), 1).astype(F32)
        allowed = col < count
        if diagonal:
            row = lax.broadcasted_iota(jnp.int32, (MOST_OWN, MOST_OWN), 0).astype(F32)
            allowed = jnp.logical_and(allowed, col <= row)

        def one(f, _):
            e = f // group
            first = pl.multiple_of(lax.rem(f, group) * MOST_OWN, MOST_OWN)
            rows = pl.ds(first, MOST_OWN)
            ecol = pl.multiple_of(e * HEAD_DIM, HEAD_DIM)
            keys = kvbuf[t, :, pl.ds(ecol, HEAD_DIM)]
            vals = kvbuf[t, :, pl.ds(e_cols + ecol, HEAD_DIM)]
            score = lax.dot_general(
                qs[e, rows, :], keys, (((1,), (1,)), ((), ())), preferred_element_type=F32
            )
            score = jnp.where(allowed, score, NEG)
            old = m_s[e, rows, :]
            top = jnp.maximum(old, jnp.max(score, axis=1, keepdims=True))
            prob = jnp.where(allowed, jnp.exp(score - top[:, :1]), 0.0)
            shrink = jnp.exp(old - top)
            m_s[e, rows, :] = top
            l_s[e, rows, :] = l_s[e, rows, :] * shrink + jnp.sum(prob, axis=1, keepdims=True)
            acc[e, rows, :] = acc[e, rows, :] * shrink + jnp.dot(
                prob.astype(BF16), vals, preferred_element_type=F32
            )
            return 0

        lax.fori_loop(0, HEADS, one, 0, unroll=4)

    def attend_past(t):
        @pl.when(t < seq)
        def _():
            attend(t, False)

    attend(seq, True)
    for k in range(1, A):
        ring_k.slow(k)
        ring_o.slow(k)
        for j in range(1, B):
            ring_k.fast(k - 1, j)
            ring_o.fast(k - 1, j)
        attend_past(ring_k.piece(k, 0))
        for j in range(1, B):
            attend_past(ring_k.piece(k - 1, j))
    for j in range(1, B):
        ring_o.fast(A - 1, j)
    ring_o.relay()
    for j in range(1, B):
        ring_k.fast(A - 1, j)
    for j in range(1, B):
        attend_past(ring_k.piece(A - 1, j))
    for head in range(HEADS):
        first = (head % group) * MOST_OWN
        rows = slice(first, first + MOST_OWN)
        total = l_s[head // group, rows, :]
        total = jnp.where(total > 0.0, total, 1.0)
        att[:, head * HEAD_DIM : (head + 1) * HEAD_DIM] = (
            acc[head // group, rows, :] / total
        ).astype(BF16)
    ring_o.gather_core()
    for s in range(n):
        blk[:, s * o_cols : (s + 1) * o_cols] = jnp.dot(
            att[...], obuf[s], preferred_element_type=F32
        ).astype(BF16)
    ring_w.finish()
    ring_k.finish()
    ring_o.finish()


def add_kernel(tile, tok, ch, gates, oh, blk, out):
    seq = lax.axis_index("seq")
    t_rows = tile * pl.num_programs(0)
    low = seq * t_rows + pl.program_id(0) * tile
    rows = lax.broadcasted_iota(jnp.int32, (tile, 1), 0) + low
    gate = jnp.sum(jnp.where(ch[...] == rows, gates[...], 0.0), axis=1, keepdims=True)
    lift = lax.dot_general(
        oh[...], blk[...], (((0,), (0,)), ((), ())), preferred_element_type=F32
    )
    out[...] = (tok[...].astype(F32) + gate * lift).astype(BF16)


def per_device(tokens, chosen, gates, w_query, w_key, w_value, w_out):
    n = lax.axis_size("seq")
    A = 4 if n % 4 == 0 else 1
    B = n // A
    t_rows, width = tokens.shape
    k_rows, q_cols = w_query.shape
    e_cols = w_key.shape[1]
    all_cols = q_cols + 2 * e_cols
    o_rows, o_cols = w_out.shape
    picks = chosen.reshape(1, -1)
    gate_row = gates.reshape(1, -1)
    dma = pltpu.SemaphoreType.DMA
    any_spec = pl.BlockSpec(memory_space=pl.ANY)
    vmem_spec = pl.BlockSpec(memory_space=pltpu.VMEM)
    steps_x = max(A * (B - 1), 1)

    def pair(count):
        return (dma((count,)), dma((count,)))

    sems = []
    for _ in range(2):
        sems += [pair(A - 1), pair(steps_x), pair(n - 1), pair(2 * (n - 1))]
    sems += [pair(A - 1), pair(steps_x)]
    flat = [x for two in sems for x in two]

    def body(*refs):
        head, tail = refs[: len(refs) - len(flat)], refs[len(refs) - len(flat) :]
        pairs = [(tail[i], tail[i + 1]) for i in range(0, len(tail), 2)]
        main_kernel(A, B, *head, *pairs)

    blk, oh = pl.pallas_call(
        body,
        out_shape=(
            jax.ShapeDtypeStruct((MOST_OWN, width), BF16),
            jax.ShapeDtypeStruct((MOST_OWN, t_rows), BF16),
        ),
        in_specs=[any_spec, vmem_spec] + [any_spec] * 4,
        out_specs=(vmem_spec, vmem_spec),
        scratch_shapes=[
            pltpu.VMEM((t_rows, width), BF16),
            pltpu.VMEM((n * k_rows, all_cols), BF16),
            pltpu.VMEM((n, o_rows, o_cols), BF16),
            pltpu.VMEM((n, MOST_OWN, 2 * e_cols), BF16),
            pltpu.VMEM((MOST_OWN, width), BF16),
            pltpu.VMEM((KV_HEADS, HEADS // KV_HEADS * MOST_OWN, HEAD_DIM), BF16),
            pltpu.VMEM((KV_HEADS, HEADS // KV_HEADS * MOST_OWN, HEAD_DIM), F32),
            pltpu.VMEM((KV_HEADS, HEADS // KV_HEADS * MOST_OWN, HEAD_DIM), F32),
            pltpu.VMEM((KV_HEADS, HEADS // KV_HEADS * MOST_OWN, HEAD_DIM), F32),
            pltpu.VMEM((MOST_OWN, HEADS * HEAD_DIM), BF16),
            dma((5,)),
            *flat,
        ],
        compiler_params=pltpu.CompilerParams(
            collective_id=0, has_side_effects=True, vmem_limit_bytes=60 * 1024 * 1024
        ),
        name="gather_attend",
    )(tokens, picks, w_query, w_key, w_value, w_out)

    tile = 256
    return pl.pallas_call(
        functools.partial(add_kernel, tile),
        grid=(t_rows // tile,),
        out_shape=jax.ShapeDtypeStruct((t_rows, width), BF16),
        in_specs=[
            pl.BlockSpec((tile, width), lambda i: (i, 0)),
            pl.BlockSpec(picks.shape, lambda i: (0, 0)),
            pl.BlockSpec(picks.shape, lambda i: (0, 0)),
            pl.BlockSpec((MOST_OWN, tile), lambda i: (0, i)),
            pl.BlockSpec((MOST_OWN, width), lambda i: (0, 0)),
        ],
        out_specs=pl.BlockSpec((tile, width), lambda i: (i, 0)),
        compiler_params=pltpu.CompilerParams(vmem_limit_bytes=62 * 1024 * 1024),
        name="add_rows",
    )(tokens, picks, gate_row, oh, blk)


def solution(mesh):
    return jax.shard_map(
        per_device,
        mesh=mesh,
        in_specs=(
            P(("dp", "seq"), None),
            P("dp"),
            P("dp"),
            P("seq", None),
            P("seq", None),
            P("seq", None),
            P(None, "seq"),
        ),
        out_specs=P(("dp", "seq"), None),
        check_vma=False,
    )
```

profile of v0, /device:TPU:27, one launch (start us, length us, event | category | flops | bytes accessed | tf_op | source)
XLA Modules:
  0.0 87.5 jit_solution(3135448673809421971)
XLA Ops:
  0.0 81.4 %gather_attend.1 = (bf16[256,2048]{1,0:T(8,128)(2,1)}, bf16[256,1024]{1,0:T(8,128)(2,1)}) custom-call(bf16[1024,2048]{1,0:T(8,128)(2,1)} %tok.1, s32[1,1024]{1,0:T(1,128)} %bitcast.2, bf16[256,1024]{1,0:T(8,128)(2,1)} %refs_2_.1, bf16[256,256]{1,0:T(8,128)(2,1)} %refs_3_.1, bf16[256,256]{1,0:T(8,128)(2,1)} %refs_4_.1, bf16[1024,256]{1,0:T(8,128)(2,1)} %refs_5_.1), custom_call_target="tpu_custom_call" | custom-call | tf_op jit(solution)/shard_map/gather_attend/pallas_call | solution.py:359
  81.4 6.1 %add_rows.1 = bf16[1024,2048]{1,0:T(8,128)(2,1)} custom-call(bf16[1024,2048]{1,0:T(8,128)(2,1)} %tok.1, s32[1,1024]{1,0:T(1,128)} %bitcast.3, f32[1,1024]{1,0:T(1,128)} %bitcast.4, bf16[256,1024]{1,0:T(8,128)(2,1)} %get-tuple-element.7.oh, bf16[256,2048]{1,0:T(8,128)(2,1)} %get-tuple-element.8.blk), custom_call_target="tpu_custom_call" | custom-call | tf_op jit(solution)/shard_map/add_rows/pallas_call | solution.py:388
where the time goes:
time: 89.1 us; the launch traced here: 87.5 us
  Pallas kernels  87.5 us (98%)
    pallas_call x1, Pallas kernels, per_device(): pl.pallas_call(body, out_shape=(jax.ShapeDtypeStruct((MOST_OWN, width), B...  81.4 us
    pallas_call x1, Pallas kernels, per_device(): pl.pallas_call(functools.partial(add_kernel, tile), grid=(t_rows // tile,...  6.1 us

commit v1 on v0

v1 whole, which is shorter than its diff:
```python
import functools

import jax
import jax.numpy as jnp
from jax import lax
from jax.experimental import pallas as pl
from jax.experimental.pallas import tpu as pltpu
from jax.sharding import PartitionSpec as P

HEADS = 8
KV_HEADS = 2
HEAD_DIM = 128
MOST_OWN = 256
ONES = 16
Q_SHARE = 9
O_SHARE = 9
MESH = pl.DeviceIdType.MESH
NEG = -1e30
F32 = jnp.float32
BF16 = jnp.bfloat16


class Ring:
    def __init__(self, geo, sems, region_in, region_y):
        self.g = geo
        self.sems = sems
        self.region_in = region_in
        self.region_y = region_y
        self.sends = []
        a_count, b_count = geo["A"], geo["B"]
        self.order = arrivals(a_count, b_count)

    def piece(self, k, j):
        return piece_of(self.g, k, j)

    def copy(self, kind, index, ref, dp, seq):
        send, recv = self.sems[kind]
        return remote(ref, send.at[index], recv.at[index], dp, seq)

    def send(self, *args):
        made = self.copy(*args)
        made.start()
        self.sends.append(made)

    def arrive(self, kind, index, ref):
        self.copy(kind, index, ref, self.g["dp"], self.g["z_next"]).wait_recv()

    def mine(self, s):
        return self.region_in(s, self.g["y"], self.g["c"])

    def send_core(self, k, j):
        g = self.g
        self.send("d", self.order.index((k, j)), self.mine(self.piece(k, j)), g["dp_c"], g["seq"])

    def send_y(self, k, j):
        g = self.g
        ref = self.region_y(self.piece(k, j), g["y"], g["c"])
        self.send("y", self.order.index((k, j)), ref, g["dp_y"], g["seq"])

    def slow(self, k):
        g = self.g
        s = self.piece(k, 0)
        if k > 0:
            self.arrive("z", k - 1, self.mine(s))
        if k < g["A"] - 1:
            self.send("z", k, self.mine(s), g["dp"], g["z_next"])
        if g["B"] > 1:
            self.send("x", k * (g["B"] - 1), self.mine(s), g["dp"], g["x_next"])
        if k > 0:
            self.send_core(k, 0)

    def fast(self, k, j):
        g = self.g
        s = self.piece(k, j)
        self.arrive("x", k * (g["B"] - 1) + j - 1, self.mine(s))
        if j < g["B"] - 1:
            self.send("x", k * (g["B"] - 1) + j, self.mine(s), g["dp"], g["x_next"])
        self.send_core(k, j)

    def relay(self, k, j):
        g = self.g
        index = self.order.index((k, j))
        ref = self.region_y(self.piece(k, j), 1 - g["y"], g["c"])
        self.arrive("y", index, ref)
        self.send("d", len(self.order) + index, ref, g["dp_c"], g["seq"])

    def from_core(self, k, j):
        g = self.g
        index = self.order.index((k, j))
        s = self.piece(k, j)
        self.arrive("d", index, self.region_in(s, g["y"], 1 - g["c"]))
        self.arrive("d", len(self.order) + index, self.region_y(s, 1 - g["y"], 1 - g["c"]))

    def finish(self):
        for made in self.sends:
            made.wait_send()


class Causal:
    def __init__(self, geo, sems, ref, parts):
        self.g = geo
        self.sems = sems
        self.ref = ref
        self.parts = parts
        self.sends = []

    def has(self, k, j):
        g = self.g
        if k > 0:
            return g["a"] >= k
        return g["b"] >= j

    def copy(self, kind, index, e, s, seq):
        send, recv = self.sems[kind]
        at = index * self.parts + e
        return remote(self.ref(s, e), send.at[at], recv.at[at], self.g["dp"], seq)

    def send(self, cond, *args):
        made = self.copy(*args)
        pl.when(cond)(made.start)
        self.sends.append((cond, made))

    def arrive(self, cond, *args):
        pl.when(cond)(self.copy(*args, self.g["z_next"]).wait_recv)

    def slow(self, k):
        g = self.g
        s = piece_of(g, k, 0)
        for e in range(self.parts):
            if k > 0:
                self.arrive(g["a"] >= k, "z", k - 1, e, s)
            if k < g["A"] - 1:
                cond = jnp.logical_and(g["a"] >= k, g["a"] + 1 < g["A"])
                self.send(cond, "z", k, e, s, g["z_next"])
            if g["B"] > 1:
                cond = g["a"] >= k if k > 0 else g["b"] + 1 < g["B"]
                self.send(cond, "x", k * (g["B"] - 1), e, s, g["x_next"])

    def fast(self, k, j):
        g = self.g
        s = piece_of(g, k, j)
        for e in range(self.parts):
            self.arrive(self.has(k, j), "x", k * (g["B"] - 1) + j - 1, e, s)
            if j < g["B"] - 1:
                cond = self.has(k, j)
                if k == 0:
                    cond = jnp.logical_and(cond, g["b"] + 1 < g["B"])
                self.send(cond, "x", k * (g["B"] - 1) + j, e, s, g["x_next"])

    def finish(self):
        for cond, made in self.sends:
            pl.when(cond)(made.wait_send)


def remote(ref, send, recv, dp, seq):
    return pltpu.make_async_remote_copy(
        src_ref=ref,
        dst_ref=ref,
        send_sem=send,
        recv_sem=recv,
        device_id=(dp, seq),
        device_id_type=MESH,
    )


def arrivals(a_count, b_count):
    order = []
    for k in range(1, a_count):
        order += [(k, 0)] + [(k - 1, j) for j in range(1, b_count)]
    return order + [(a_count - 1, j) for j in range(1, b_count)]


def piece_of(g, k, j):
    a = lax.rem(g["a"] - k + g["A"], g["A"])
    b = lax.rem(g["b"] - j + g["B"], g["B"])
    return a * g["B"] + b


def up16(value):
    return (value + 15) // 16 * 16


def main_kernel(
    A, B, tok, ch, wq, wk, wv, wo, blk, oh_out,
    tok_v, kvw, qw, obuf, kv, normed, qt, acc, m_s, counts, att, lsem,
    wz, wx, wy, wd, qz, qx, qy, qd, oz, ox, oy, od, kz, kx,
):
    n = A * B
    dp = lax.axis_index("dp")
    seq = lax.axis_index("seq")
    a, b = seq // B, lax.rem(seq, B)
    y, c = lax.rem(dp // 2, 2), lax.rem(dp, 2)
    z_next = lax.rem(a + 1, A) * B + b
    z_prev = lax.rem(a + A - 1, A) * B + b
    x_next = a * B + lax.rem(b + 1, B)
    x_prev = a * B + lax.rem(b + B - 1, B)
    dp_y = dp + 2 * (1 - 2 * y)
    dp_c = dp + 1 - 2 * c
    geo = dict(
        A=A, B=B, a=a, b=b, y=y, c=c, dp=dp, seq=seq,
        z_next=z_next, x_next=x_next, dp_y=dp_y, dp_c=dp_c,
    )
    t_rows = tok.shape[0]
    width = tok.shape[1]
    k_rows = wq.shape[0]
    q_cols, e_cols = wq.shape[1], wk.shape[1]
    o_rows, o_cols = wo.shape
    group = HEADS // KV_HEADS
    pair = 2 * HEAD_DIM

    rows_here = pl.ds(pl.multiple_of(seq * k_rows, k_rows), k_rows)
    local = []
    for e in range(KV_HEADS):
        cols = pl.ds(e * HEAD_DIM, HEAD_DIM)
        local.append((wk.at[:, cols], kvw.at[rows_here, pl.ds(e * pair, HEAD_DIM)]))
        local.append((wv.at[:, cols], kvw.at[rows_here, pl.ds(e * pair + HEAD_DIM, HEAD_DIM)]))
    local += [(wq, qw.at[rows_here, :]), (tok, tok_v), (wo, obuf.at[seq])]
    local = [pltpu.make_async_copy(s, d, lsem.at[i]) for i, (s, d) in enumerate(local)]
    for made in local:
        made.start()
    load_kv, (load_q, load_tok, load_o) = local[: 2 * KV_HEADS], local[2 * KV_HEADS :]

    greet = [(dp, z_next)] + ([(dp, z_prev)] if A > 2 else [])
    if B > 1:
        greet += [(dp, x_next)] + ([(dp, x_prev)] if B > 2 else [])
    greet += [(dp_y, seq), (dp_c, seq)]
    barrier = pltpu.get_barrier_semaphore()
    for who in greet:
        pl.semaphore_signal(barrier, inc=1, device_id=who, device_id_type=MESH)
    pl.semaphore_wait(barrier, len(greet))

    quarter = 2 * e_cols // 4

    def w_region(s, y, c):
        return kvw.at[
            pl.ds(pl.multiple_of(s * k_rows, k_rows), k_rows),
            pl.ds(pl.multiple_of((2 * c + y) * quarter, 128), quarter),
        ]

    q_half = q_cols // 2
    q_in = up16(k_rows * Q_SHARE // 16)

    def q_region(s, c, start, size):
        return qw.at[
            pl.ds(pl.multiple_of(s * k_rows + start, 16), size),
            pl.ds(pl.multiple_of(c * q_half, 128), q_half),
        ]

    o_half = o_rows // 2
    o_in = up16(o_half * O_SHARE // 16)

    def o_region(s, start, size):
        return obuf.at[s, pl.ds(pl.multiple_of(start, 16), size), :]

    W = Ring(geo, {"z": wz, "x": wx, "y": wy, "d": wd}, w_region, w_region)
    Q = Ring(
        geo,
        {"z": qz, "x": qx, "y": qy, "d": qd},
        lambda s, y, c: q_region(s, c, y * (k_rows - q_in), q_in),
        lambda s, y, c: q_region(s, c, y * q_in, k_rows - q_in),
    )
    O = Ring(
        geo,
        {"z": oz, "x": ox, "y": oy, "d": od},
        lambda s, y, c: o_region(s, c * o_half + y * (o_half - o_in), o_in),
        lambda s, y, c: o_region(s, c * o_half + y * o_in, o_half - o_in),
    )
    K = Causal(geo, {"z": kz, "x": kx}, lambda s, e: kv.at[s, e], KV_HEADS)
    order = W.order

    for made in load_kv:
        made.wait()
    W.slow(0)
    load_q.wait()
    Q.slow(0)

    def gather():
        base = seq * t_rows
        picks = ch[...]
        start = jnp.sum((picks < base).astype(F32), axis=1, keepdims=True)
        rel = picks - base
        inside = (rel >= 0) & (rel < t_rows)
        place = jnp.where(inside, (rel + 1).astype(F32), 0.0)
        rank = lax.broadcasted_iota(jnp.int32, picks.shape, 1).astype(F32) - start
        slots = lax.broadcasted_iota(jnp.int32, (MOST_OWN, 1), 0).astype(F32)
        own = jnp.sum(jnp.where(rank == slots, place, 0.0), axis=1, keepdims=True) - 1.0
        spots = lax.broadcasted_iota(jnp.int32, (1, t_rows), 1).astype(F32)
        oh_out[...] = (own == spots).astype(F32).astype(BF16)
        for t in range(n):
            held = (picks >= t * t_rows) & (picks < (t + 1) * t_rows)
            count = jnp.sum(held.astype(F32), axis=1, keepdims=True)
            counts[t] = jnp.broadcast_to(count, (1, HEAD_DIM))
        load_tok.wait()
        chunk = 512
        square = jnp.zeros((MOST_OWN, 1), F32)
        for i in range(width // chunk):
            cols = slice(i * chunk, (i + 1) * chunk)
            rows = jnp.dot(oh_out[...], tok_v[:, cols], preferred_element_type=F32)
            square = square + jnp.sum(rows * rows, axis=1, keepdims=True)
            normed[:, cols] = rows.astype(BF16)
        scale = lax.rsqrt(square / width + 1e-06)
        for i in range(width // chunk):
            cols = slice(i * chunk, (i + 1) * chunk)
            normed[:, cols] = (normed[:, cols].astype(F32) * scale).astype(BF16)

    def project_kv():
        for e in range(KV_HEADS):
            part = jnp.dot(
                normed[...], kvw[:, e * pair : (e + 1) * pair], preferred_element_type=F32
            )
            kv[seq, e, 0] = part[:, :HEAD_DIM].astype(BF16)
            flip = part[:, HEAD_DIM:].T.astype(BF16)
            kv[seq, e, 1, :HEAD_DIM, :] = flip[:, :HEAD_DIM]
            kv[seq, e, 1, HEAD_DIM:, :] = flip[:, HEAD_DIM:]

    def project_q():
        for i in range(HEADS // 2):
            part = jnp.dot(
                normed[...], qw[:, i * pair : (i + 1) * pair], preferred_element_type=F32
            )
            part = part * HEAD_DIM**-0.5
            for h in range(2):
                head = i * 2 + h
                e, first = head // group, (head % group) * MOST_OWN
                flip = part[:, h * HEAD_DIM : (h + 1) * HEAD_DIM].T.astype(BF16)
                qt[e, :HEAD_DIM, first : first + MOST_OWN] = flip
        row = lax.broadcasted_iota(jnp.int32, (HEAD_DIM, group * MOST_OWN), 0)
        for e in range(KV_HEADS):
            qt[e, HEAD_DIM:, :] = (row == 0).astype(F32).astype(BF16)

    def attend(t, diagonal):
        row = lax.broadcasted_iota(jnp.int32, (MOST_OWN, HEAD_DIM), 0).astype(F32)
        bias = jnp.where(row < counts[t], 0.0, NEG).astype(BF16)
        ones = jnp.ones((ONES, MOST_OWN), BF16)
        heads = range(HEADS)
        left, right = [], []
        for e in range(KV_HEADS):
            left.append(jnp.concatenate([kv[t, e, 0], bias], axis=1))
            flip = [kv[t, e, 1, :HEAD_DIM, :], kv[t, e, 1, HEAD_DIM:, :]]
            right.append(jnp.concatenate([jnp.concatenate(flip, axis=1), ones], axis=0))
        score = []
        for f in heads:
            first = (f % group) * MOST_OWN
            query = qt[f // group, :, first : first + MOST_OWN]
            score.append(jnp.dot(left[f // group], query, preferred_element_type=F32))
        if diagonal:
            key = lax.broadcasted_iota(jnp.int32, (MOST_OWN, MOST_OWN), 0)
            asks = lax.broadcasted_iota(jnp.int32, (MOST_OWN, MOST_OWN), 1)
            score = [jnp.where(key <= asks, s, NEG) for s in score]
            top = [jnp.max(s, axis=0, keepdims=True) for s in score]
        else:
            old = [m_s[f] for f in heads]
            held = [acc[f] for f in heads]
            top = [
                jnp.maximum(o, jnp.max(s, axis=0, keepdims=True)) for o, s in zip(old, score)
            ]
        prob = [jnp.exp(s - m).astype(BF16) for s, m in zip(score, top)]
        new = [
            jnp.dot(right[f // group], prob[f], preferred_element_type=F32) for f in heads
        ]
        if not diagonal:
            new = [h * jnp.exp(o - m) + v for h, o, m, v in zip(held, old, top, new)]
        for f in heads:
            m_s[f] = top[f]
            acc[f] = new[f]

    def attend_past(k, j):
        pl.when(K.has(k, j))(lambda: attend(piece_of(geo, k, j), False))

    waiting = []

    def pump(count):
        for _ in range(min(count, len(waiting))):
            ring, k, j = waiting.pop(0)
            ring.send_y(k, j)

    def step(ring, k):
        got = []
        if k < A:
            ring.slow(k)
            got.append((k, 0))
        for j in range(1, B):
            ring.fast(k - 1, j)
            got.append((k - 1, j))
        waiting.extend((ring, *kj) for kj in got)
        return got

    gather()
    before = []
    for k in range(1, A + 1):
        kept, waiting[:] = waiting[:], []
        got = step(W, k)
        pump(len(got))
        waiting.extend(kept)
        for kj in before:
            W.relay(*kj)
        before = got
        step(Q, k)
        if k < A:
            pump(1)
        if k == max(A - 1, 1):
            load_o.wait()
            O.slow(0)
    pump(len(waiting))
    for kj in before:
        W.relay(*kj)
    for kj in order:
        W.from_core(*kj)
    project_kv()
    K.slow(0)
    step(O, 1)
    pump(len(waiting))
    if A > 1:
        K.slow(1)
    for j in range(1, B):
        K.fast(0, j)
    if A > 1:
        step(O, 2)
        pump(len(waiting))
    for kj in order:
        Q.relay(*kj)
    for kj in order:
        Q.from_core(*kj)
    project_q()
    attend(seq, True)
    for k in range(1, A):
        if k + 1 < A:
            K.slow(k + 1)
        for j in range(1, B):
            K.fast(k, j)
        attend_past(k, 0)
        for j in range(1, B):
            attend_past(k - 1, j)
        if k + 2 <= A:
            step(O, k + 2)
            pump(len(waiting))
    for j in range(1, B):
        attend_past(A - 1, j)
    for kj in order:
        O.relay(*kj)
    for f in range(HEADS):
        total = acc[f]
        flip = (total[:HEAD_DIM] / total[HEAD_DIM : HEAD_DIM + 1]).T
        att[:, f * HEAD_DIM : (f + 1) * HEAD_DIM] = flip.astype(BF16)

    def project_out(s):
        cols = pl.ds(pl.multiple_of(s * o_cols, o_cols), o_cols)
        blk[:, cols] = jnp.dot(att[...], obuf[s], preferred_element_type=F32).astype(BF16)

    if o_cols % 128 == 0:
        project_out(seq)
    for kj in order:
        O.from_core(*kj)
        if o_cols % 128 == 0:
            project_out(piece_of(geo, *kj))
    if o_cols % 128 != 0:
        for s in range(n):
            blk[:, s * o_cols : (s + 1) * o_cols] = jnp.dot(
                att[...], obuf[s], preferred_element_type=F32
            ).astype(BF16)
    for ring in (W, Q, O, K):
        ring.finish()


def add_kernel(tile, tok, ch, gates, oh, blk, out):
    seq = lax.axis_index("seq")
    t_rows = tile * pl.num_programs(0)
    low = seq * t_rows + pl.program_id(0) * tile
    rows = lax.broadcasted_iota(jnp.int32, (tile, 1), 0) + low
    gate = jnp.sum(jnp.where(ch[...] == rows, gates[...], 0.0), axis=1, keepdims=True)
    lift = lax.dot_general(
        oh[...], blk[...], (((0,), (0,)), ((), ())), preferred_element_type=F32
    )
    out[...] = (tok[...].astype(F32) + gate * lift).astype(BF16)


def per_device(tokens, chosen, gates, w_query, w_key, w_value, w_out):
    n = lax.axis_size("seq")
    A = 4 if n % 4 == 0 else 1
    B = n // A
    t_rows, width = tokens.shape
    k_rows, q_cols = w_query.shape
    e_cols = w_key.shape[1]
    o_rows, o_cols = w_out.shape
    picks = chosen.reshape(1, -1)
    gate_row = gates.reshape(1, -1)
    dma = pltpu.SemaphoreType.DMA
    any_spec = pl.BlockSpec(memory_space=pl.ANY)
    vmem_spec = pl.BlockSpec(memory_space=pltpu.VMEM)
    steps_x = max(A * (B - 1), 1)
    steps_z = max(A - 1, 1)

    def pair(count):
        return (dma((count,)), dma((count,)))

    sems = []
    for _ in range(3):
        sems += [pair(steps_z), pair(steps_x), pair(n - 1), pair(2 * (n - 1))]
    sems += [pair(KV_HEADS * steps_z), pair(KV_HEADS * steps_x)]
    flat = [x for two in sems for x in two]

    def body(*refs):
        head, tail = refs[: len(refs) - len(flat)], refs[len(refs) - len(flat) :]
        pairs = [(tail[i], tail[i + 1]) for i in range(0, len(tail), 2)]
        main_kernel(A, B, *head, *pairs)

    blk, oh = pl.pallas_call(
        body,
        out_shape=(
            jax.ShapeDtypeStruct((MOST_OWN, width), BF16),
            jax.ShapeDtypeStruct((MOST_OWN, t_rows), BF16),
        ),
        in_specs=[any_spec, vmem_spec] + [any_spec] * 4,
        out_specs=(vmem_spec, vmem_spec),
        scratch_shapes=[
            pltpu.VMEM((t_rows, width), BF16),
            pltpu.VMEM((n * k_rows, 2 * e_cols), BF16),
            pltpu.VMEM((n * k_rows, q_cols), BF16),
            pltpu.VMEM((n, o_rows, o_cols), BF16),
            pltpu.VMEM((n, KV_HEADS, 2, MOST_OWN, HEAD_DIM), BF16),
            pltpu.VMEM((MOST_OWN, width), BF16),
            pltpu.VMEM((KV_HEADS, 2 * HEAD_DIM, HEADS // KV_HEADS * MOST_OWN), BF16),
            pltpu.VMEM((HEADS, HEAD_DIM + ONES, MOST_OWN), F32),
            pltpu.VMEM((HEADS, 1, MOST_OWN), F32),
            pltpu.VMEM((n, 1, HEAD_DIM), F32),
            pltpu.VMEM((MOST_OWN, HEADS * HEAD_DIM), BF16),
            dma((2 * KV_HEADS + 3,)),
            *flat,
        ],
        compiler_params=pltpu.CompilerParams(
            collective_id=0, has_side_effects=True, vmem_limit_bytes=60 * 1024 * 1024
        ),
        name="gather_attend",
    )(tokens, picks, w_query, w_key, w_value, w_out)

    tile = 256
    return pl.pallas_call(
        functools.partial(add_kernel, tile),
        grid=(t_rows // tile,),
        out_shape=jax.ShapeDtypeStruct((t_rows, width), BF16),
        in_specs=[
            pl.BlockSpec((tile, width), lambda i: (i, 0)),
            pl.BlockSpec(picks.shape, lambda i: (0, 0)),
            pl.BlockSpec(picks.shape, lambda i: (0, 0)),
            pl.BlockSpec((MOST_OWN, tile), lambda i: (0, i)),
            pl.BlockSpec((MOST_OWN, width), lambda i: (0, 0)),
        ],
        out_specs=pl.BlockSpec((tile, width), lambda i: (i, 0)),
        compiler_params=pltpu.CompilerParams(vmem_limit_bytes=62 * 1024 * 1024),
        name="add_rows",
    )(tokens, picks, gate_row, oh, blk)


def solution(mesh):
    return jax.shard_map(
        per_device,
        mesh=mesh,
        in_specs=(
            P(("dp", "seq"), None),
            P("dp"),
            P("dp"),
            P("seq", None),
            P("seq", None),
            P("seq", None),
            P(None, "seq"),
        ),
        out_specs=P(("dp", "seq"), None),
        check_vma=False,
    )
```

time: 89.1 us -> 77.7 us (0.87); the launches traced: 87.5 us -> 77.5 us
  Pallas kernels: 87.5 us -> 77.5 us
    pallas_call x1, Pallas kernels: 81.4 us -> 71.4 us  [per_device(): pl.pallas_call(body, out_shape=(jax.ShapeDtypeStruct((MOST_OWN, width), B...]
where the time goes in v1:
time: 77.7 us; the launch traced here: 77.5 us
  Pallas kernels  77.5 us (100%)
    pallas_call x1, Pallas kernels, per_device(): pl.pallas_call(body, out_shape=(jax.ShapeDtypeStruct((MOST_OWN, width), B...  71.4 us
    pallas_call x1, Pallas kernels, per_device(): pl.pallas_call(functools.partial(add_kernel, tile), grid=(t_rows // tile,...  6.1 us

profile of v1, /device:TPU:27, one launch (start us, length us, event | category | flops | bytes accessed | tf_op | source)
XLA Modules:
  0.0 77.5 jit_solution(6385934536474514011)
XLA Ops:
  0.0 71.4 %gather_attend.1 = (bf16[256,2048]{1,0:T(8,128)(2,1)}, bf16[256,1024]{1,0:T(8,128)(2,1)}) custom-call(bf16[1024,2048]{1,0:T(8,128)(2,1)} %tok.1, s32[1,1024]{1,0:T(1,128)} %bitcast.2, bf16[256,1024]{1,0:T(8,128)(2,1)} %refs_2_.1, bf16[256,256]{1,0:T(8,128)(2,1)} %refs_3_.1, bf16[256,256]{1,0:T(8,128)(2,1)} %refs_4_.1, bf16[1024,256]{1,0:T(8,128)(2,1)} %refs_5_.1), custom_call_target="tpu_custom_call" | custom-call | tf_op jit(solution)/shard_map/gather_attend/pallas_call | solution.py:507
  71.4 6.1 %add_rows.1 = bf16[1024,2048]{1,0:T(8,128)(2,1)} custom-call(bf16[1024,2048]{1,0:T(8,128)(2,1)} %tok.1, s32[1,1024]{1,0:T(1,128)} %bitcast.3, f32[1,1024]{1,0:T(1,128)} %bitcast.4, bf16[256,1024]{1,0:T(8,128)(2,1)} %get-tuple-element.7.oh, bf16[256,2048]{1,0:T(8,128)(2,1)} %get-tuple-element.8.blk), custom_call_target="tpu_custom_call" | custom-call | tf_op jit(solution)/shard_map/add_rows/pallas_call | solution.py:537

commit v2 on v1

--- a/solution.py
+++ b/solution.py
@@ -12,8 +12,40 @@
 HEAD_DIM = 128
 MOST_OWN = 256
 ONES = 16
+TILES = 4
+ADD_TILES = 4
+MAIN_VMEM = 36
+ADD_VMEM = 12
 Q_SHARE = 9
-O_SHARE = 9
+O_SHARE = 17
+PLAN = (
+    ("W", "oz", 0, 0), ("Q", "ox", 0, 0), ("W", "ox", 0, 0), ("Q", "oz", 0, 0), ("gather",),
+    ("W", "z", 1, 0), ("W", "ys", 1, 0), ("O", "ox", 0, 0), ("gates", 0), ("Q", "x", 0, 1),
+    ("Q", "ys", 0, 1), ("Q", "z", 1, 0), ("gates", 1), ("Q", "ys", 1, 0), ("W", "x", 1, 1),
+    ("W", "z", 2, 0), ("gates", 2), ("W", "ys", 2, 0), ("O", "oz", 0, 0), ("W", "ys", 1, 1),
+    ("gates", 3), ("W", "x", 0, 1), ("W", "ys", 0, 1), ("W", "y", 1, 0), ("W", "z", 3, 0),
+    ("Q", "z", 2, 0), ("W", "ys", 3, 0), ("W", "x", 2, 1), ("W", "ys", 2, 1), ("Q", "y", 0, 1),
+    ("Q", "ys", 2, 0), ("W", "y", 0, 1), ("O", "x", 0, 1), ("O", "z", 1, 0), ("W", "x", 3, 1),
+    ("W", "y", 3, 0), ("Q", "x", 1, 1), ("W", "e", 0, 1), ("Q", "y", 1, 0), ("W", "ys", 3, 1),
+    ("Q", "z", 3, 0), ("W", "y", 2, 0), ("W", "y", 1, 1), ("Q", "ys", 1, 1), ("W", "y", 2, 1),
+    ("W", "e", 1, 0), ("W", "e", 3, 0), ("Q", "ys", 3, 0), ("Q", "x", 2, 1), ("O", "z", 2, 0),
+    ("W", "y", 3, 1), ("W", "e", 2, 1), ("O", "ys", 2, 0), ("W", "e", 2, 0), ("W", "e", 1, 1),
+    ("W", "e", 3, 1), ("kv",), ("K", "z", 0, 0, 1), ("Q", "x", 3, 1), ("K", "z", 0, 0, 0),
+    ("Q", "ys", 3, 1), ("Q", "ys", 2, 1), ("Q", "e", 0, 1), ("Q", "e", 1, 0), ("O", "z", 3, 0),
+    ("Q", "y", 1, 1), ("Q", "y", 2, 0), ("O", "ys", 1, 0), ("K", "z", 1, 0, 1), ("O", "x", 2, 1),
+    ("K", "z", 1, 0, 0), ("Q", "y", 2, 1), ("O", "ys", 0, 1), ("Q", "y", 3, 0), ("O", "ys", 3, 0),
+    ("O", "ys", 2, 1), ("K", "z", 2, 0, 1), ("Q", "y", 3, 1), ("O", "y", 2, 0), ("O", "x", 1, 1),
+    ("O", "x", 3, 1), ("Q", "e", 1, 1), ("Q", "e", 2, 0), ("Q", "e", 3, 0), ("Q", "e", 2, 1),
+    ("Q", "e", 3, 1), ("K", "z", 2, 0, 0), ("O", "y", 1, 0), ("q",), ("K", "x", 0, 1, 1),
+    ("O", "e", 2, 0), ("O", "y", 0, 1), ("O", "ys", 3, 1), ("O", "e", 1, 0), ("O", "ys", 1, 1),
+    ("K", "z", 3, 0, 1), ("K", "x", 0, 1, 0), ("own",), ("O", "e", 0, 1), ("att", 1, 0),
+    ("K", "x", 2, 1, 1), ("O", "y", 3, 0), ("K", "z", 3, 0, 0), ("att", 3, 0), ("att", 0, 1),
+    ("O", "y", 2, 1), ("K", "x", 3, 1, 1), ("att", 2, 0), ("K", "x", 2, 1, 0), ("att", 2, 1),
+    ("K", "x", 1, 1, 1), ("O", "y", 3, 1), ("O", "e", 3, 0), ("O", "e", 2, 1), ("K", "x", 3, 1, 0),
+    ("att", 3, 1), ("K", "x", 1, 1, 0), ("att", 1, 1), ("norm",), ("out", 0, 0), ("out", 2, 1),
+    ("O", "y", 1, 1), ("out", 3, 0), ("out", 0, 1), ("O", "e", 3, 1), ("out", 3, 1), ("out", 2, 0),
+    ("out", 1, 0), ("O", "e", 1, 1), ("out", 1, 1),
+)
 MESH = pl.DeviceIdType.MESH
 NEG = -1e30
 F32 = jnp.float32
@@ -57,17 +89,22 @@
         ref = self.region_y(self.piece(k, j), g["y"], g["c"])
         self.send("y", self.order.index((k, j)), ref, g["dp_y"], g["seq"])
 
+    def send_z(self, k):
+        g = self.g
+        if k < g["A"] - 1:
+            self.send("z", k, self.mine(self.piece(k, 0)), g["dp"], g["z_next"])
+
+    def send_x(self, k):
+        g = self.g
+        if g["B"] > 1:
+            ref = self.mine(self.piece(k, 0))
+            self.send("x", k * (g["B"] - 1), ref, g["dp"], g["x_next"])
+
     def slow(self, k):
-        g = self.g
-        s = self.piece(k, 0)
-        if k > 0:
-            self.arrive("z", k - 1, self.mine(s))
-        if k < g["A"] - 1:
-            self.send("z", k, self.mine(s), g["dp"], g["z_next"])
-        if g["B"] > 1:
-            self.send("x", k * (g["B"] - 1), self.mine(s), g["dp"], g["x_next"])
-        if k > 0:
-            self.send_core(k, 0)
+        self.arrive("z", k - 1, self.mine(self.piece(k, 0)))
+        self.send_z(k)
+        self.send_x(k)
+        self.send_core(k, 0)
 
     def fast(self, k, j):
         g = self.g
@@ -103,6 +140,8 @@
         self.ref = ref
         self.parts = parts
         self.sends = []
+        self.detour = geo["B"] == 2 and geo["A"] >= 2
+        self.last = geo["a"] == geo["A"] - 1
 
     def has(self, k, j):
         g = self.g
@@ -123,29 +162,39 @@
     def arrive(self, cond, *args):
         pl.when(cond)(self.copy(*args, self.g["z_next"]).wait_recv)
 
-    def slow(self, k):
+    def slow(self, k, e):
         g = self.g
         s = piece_of(g, k, 0)
-        for e in range(self.parts):
-            if k > 0:
-                self.arrive(g["a"] >= k, "z", k - 1, e, s)
-            if k < g["A"] - 1:
-                cond = jnp.logical_and(g["a"] >= k, g["a"] + 1 < g["A"])
-                self.send(cond, "z", k, e, s, g["z_next"])
-            if g["B"] > 1:
-                cond = g["a"] >= k if k > 0 else g["b"] + 1 < g["B"]
-                self.send(cond, "x", k * (g["B"] - 1), e, s, g["x_next"])
-
-    def fast(self, k, j):
+        if k > 0:
+            self.arrive(g["a"] >= k, "z", k - 1, e, s)
+        if k < g["A"] - 1:
+            cond = jnp.logical_and(g["a"] >= k, g["a"] + 1 < g["A"])
+            self.send(cond, "z", k, e, s, g["z_next"])
+        if g["B"] > 1:
+            cond = g["a"] >= k if k > 0 else g["b"] + 1 < g["B"]
+            if self.detour and k == 1:
+                turned = jnp.logical_and(self.last, g["b"] == 0)
+                cond = jnp.logical_and(cond, jnp.logical_not(turned))
+            self.send(cond, "x", k * (g["B"] - 1), e, s, g["x_next"])
+
+    def fast(self, k, j, e):
         g = self.g
         s = piece_of(g, k, j)
-        for e in range(self.parts):
-            self.arrive(self.has(k, j), "x", k * (g["B"] - 1) + j - 1, e, s)
-            if j < g["B"] - 1:
-                cond = self.has(k, j)
-                if k == 0:
-                    cond = jnp.logical_and(cond, g["b"] + 1 < g["B"])
-                self.send(cond, "x", k * (g["B"] - 1) + j, e, s, g["x_next"])
+        index = k * (g["B"] - 1) + j - 1
+        has = self.has(k, j)
+        if self.detour and k == 1:
+            turned = jnp.logical_and(self.last, g["b"] == 1)
+            self.arrive(turned, "t", 0, e, s)
+            has = jnp.logical_and(has, jnp.logical_not(turned))
+        self.arrive(has, "x", index, e, s)
+        if self.detour and k == 0:
+            cond = jnp.logical_and(g["a"] == g["A"] - 2, g["b"] == 1)
+            self.send(cond, "t", 0, e, s, g["z_next"])
+        if j < g["B"] - 1:
+            cond = self.has(k, j)
+            if k == 0:
+                cond = jnp.logical_and(cond, g["b"] + 1 < g["B"])
+            self.send(cond, "x", index + 1, e, s, g["x_next"])
 
     def finish(self):
         for cond, made in self.sends:
@@ -176,14 +225,41 @@
     return a * g["B"] + b
 
 
+def plan_of(A, B):
+    if (A, B) == (4, 2):
+        return PLAN
+    order = arrivals(A, B)
+    taken = {kj: ("z" if kj[1] == 0 else "x", *kj) for kj in order}
+    parts = range(KV_HEADS)
+    plan = [("W", "oz", 0, 0), ("W", "ox", 0, 0), ("Q", "oz", 0, 0), ("Q", "ox", 0, 0), ("gather",)]
+    for what in "WQ":
+        for kj in order:
+            plan += [(what, *taken[kj]), (what, "ys", *kj)]
+    plan += [("O", "oz", 0, 0), ("O", "ox", 0, 0)]
+    plan += [("W", "y", *kj) for kj in order] + [("W", "e", *kj) for kj in order]
+    plan += [("gates", i) for i in range(TILES)] + [("kv",)] + [("K", "z", 0, 0, e) for e in parts]
+    for kj in order[: len(order) // 2]:
+        plan += [("O", *taken[kj]), ("O", "ys", *kj)]
+    plan += [("Q", "y", *kj) for kj in order] + [("Q", "e", *kj) for kj in order]
+    plan += [("q",), ("own",)]
+    for i, kj in enumerate(order):
+        plan += [("K", *taken[kj], e) for e in parts] + [("att", *kj)]
+        if i >= len(order) // 2:
+            plan += [("O", *taken[kj]), ("O", "ys", *kj)]
+    plan += [("O", "y", *kj) for kj in order] + [("norm",), ("out", 0, 0)]
+    for kj in order:
+        plan += [("O", "e", *kj), ("out", *kj)]
+    return plan
+
+
 def up16(value):
     return (value + 15) // 16 * 16
 
 
 def main_kernel(
-    A, B, tok, ch, wq, wk, wv, wo, blk, oh_out,
-    tok_v, kvw, qw, obuf, kv, normed, qt, acc, m_s, counts, att, lsem,
-    wz, wx, wy, wd, qz, qx, qy, qd, oz, ox, oy, od, kz, kx,
+    A, B, tok, ch_in, gates_in, wq, wk, wv, wo, blk, oh_out, gate_out,
+    ch, gates, oh, tok_v, kvw, qw, obuf, kv, normed, qt, acc, m_s, counts, att, lsem,
+    wz, wx, wy, wd, qz, qx, qy, qd, oz, ox, oy, od, kz, kx, kt,
 ):
     n = A * B
     dp = lax.axis_index("dp")
@@ -214,11 +290,13 @@
         cols = pl.ds(e * HEAD_DIM, HEAD_DIM)
         local.append((wk.at[:, cols], kvw.at[rows_here, pl.ds(e * pair, HEAD_DIM)]))
         local.append((wv.at[:, cols], kvw.at[rows_here, pl.ds(e * pair + HEAD_DIM, HEAD_DIM)]))
-    local += [(wq, qw.at[rows_here, :]), (tok, tok_v), (wo, obuf.at[seq])]
+    local += [(wq, qw.at[rows_here, :]), (ch_in, ch), (tok, tok_v), (wo, obuf.at[seq])]
+    local += [(gates_in, gates)]
     local = [pltpu.make_async_copy(s, d, lsem.at[i]) for i, (s, d) in enumerate(local)]
     for made in local:
         made.start()
-    load_kv, (load_q, load_tok, load_o) = local[: 2 * KV_HEADS], local[2 * KV_HEADS :]
+    load_kv, rest = local[: 2 * KV_HEADS], local[2 * KV_HEADS :]
+    load_q, load_ch, load_tok, load_o, load_gates = rest
 
     greet = [(dp, z_next)] + ([(dp, z_prev)] if A > 2 else [])
     if B > 1:
@@ -247,7 +325,7 @@
         ]
 
     o_half = o_rows // 2
-    o_in = up16(o_half * O_SHARE // 16)
+    o_in = up16(o_half * O_SHARE // 32)
 
     def o_region(s, start, size):
         return obuf.at[s, pl.ds(pl.multiple_of(start, 16), size), :]
@@ -265,16 +343,14 @@
         lambda s, y, c: o_region(s, c * o_half + y * (o_half - o_in), o_in),
         lambda s, y, c: o_region(s, c * o_half + y * o_in, o_half - o_in),
     )
-    K = Causal(geo, {"z": kz, "x": kx}, lambda s, e: kv.at[s, e], KV_HEADS)
-    order = W.order
-
-    for made in load_kv:
-        made.wait()
-    W.slow(0)
-    load_q.wait()
-    Q.slow(0)
+    K = Causal(geo, {"z": kz, "x": kx, "t": kt}, lambda s, e: kv.at[s, e], KV_HEADS)
+
+    rings = {"W": W, "Q": Q, "O": O}
+    loads = {"W": load_kv, "Q": [load_q], "O": [load_o]}
 
     def gather():
+        load_ch.wait()
+        load_gates.wait()
         base = seq * t_rows
         picks = ch[...]
         start = jnp.sum((picks < base).astype(F32), axis=1, keepdims=True)
@@ -285,23 +361,32 @@
         slots = lax.broadcasted_iota(jnp.int32, (MOST_OWN, 1), 0).astype(F32)
         own = jnp.sum(jnp.where(rank == slots, place, 0.0), axis=1, keepdims=True) - 1.0
         spots = lax.broadcasted_iota(jnp.int32, (1, t_rows), 1).astype(F32)
-        oh_out[...] = (own == spots).astype(F32).astype(BF16)
+        oh[...] = (own == spots).astype(F32)
         for t in range(n):
             held = (picks >= t * t_rows) & (picks < (t + 1) * t_rows)
             count = jnp.sum(held.astype(F32), axis=1, keepdims=True)
             counts[t] = jnp.broadcast_to(count, (1, HEAD_DIM))
         load_tok.wait()
+        hot = oh[...].astype(BF16)
         chunk = 512
         square = jnp.zeros((MOST_OWN, 1), F32)
         for i in range(width // chunk):
             cols = slice(i * chunk, (i + 1) * chunk)
-            rows = jnp.dot(oh_out[...], tok_v[:, cols], preferred_element_type=F32)
+            rows = jnp.dot(hot, tok_v[:, cols], preferred_element_type=F32)
             square = square + jnp.sum(rows * rows, axis=1, keepdims=True)
             normed[:, cols] = rows.astype(BF16)
         scale = lax.rsqrt(square / width + 1e-06)
         for i in range(width // chunk):
             cols = slice(i * chunk, (i + 1) * chunk)
             normed[:, cols] = (normed[:, cols].astype(F32) * scale).astype(BF16)
+
+    def place_gates(i):
+        tile = t_rows // TILES
+        low = i * tile
+        oh_out[low : low + tile, :] = oh[:, low : low + tile].T.astype(BF16)
+        spot = lax.broadcasted_iota(jnp.int32, (tile, 1), 0) + (seq * t_rows + low)
+        gate = jnp.sum(jnp.where(ch[...] == spot, gates[...], 0.0), axis=1, keepdims=True)
+        gate_out[low : low + tile, :] = jnp.broadcast_to(gate, (tile, HEAD_DIM))
 
     def project_kv():
         for e in range(KV_HEADS):
@@ -367,92 +452,61 @@
     def attend_past(k, j):
         pl.when(K.has(k, j))(lambda: attend(piece_of(geo, k, j), False))
 
-    waiting = []
-
-    def pump(count):
-        for _ in range(min(count, len(waiting))):
-            ring, k, j = waiting.pop(0)
+    def finish_attention():
+        for f in range(HEADS):
+            total = acc[f]
+            flip = (total[:HEAD_DIM] / total[HEAD_DIM : HEAD_DIM + 1]).T
+            att[:, f * HEAD_DIM : (f + 1) * HEAD_DIM] = flip.astype(BF16)
+
+    def project_out(k, j):
+        if o_cols % 128 == 0:
+            s = piece_of(geo, k, j)
+            cols = pl.ds(pl.multiple_of(s * o_cols, o_cols), o_cols)
+            blk[:, cols] = jnp.dot(
+                att[...], obuf[s], preferred_element_type=F32
+            ).astype(BF16)
+
+    tasks = {
+        "gather": gather,
+        "gates": place_gates,
+        "kv": project_kv,
+        "q": project_q,
+        "own": lambda: attend(seq, True),
+        "att": attend_past,
+        "norm": finish_attention,
+        "out": project_out,
+    }
+    for what, *at in plan_of(A, B):
+        if what in tasks:
+            tasks[what](*at)
+            continue
+        if what == "K":
+            kind, k, j, e = at
+            if kind == "z":
+                K.slow(k, e)
+            else:
+                K.fast(k, j, e)
+            continue
+        ring = rings[what]
+        kind, k, j = at
+        if kind in ("oz", "ox"):
+            for made in loads[what]:
+                made.wait()
+            loads[what] = []
+        if kind == "oz":
+            ring.send_z(0)
+        elif kind == "ox":
+            ring.send_x(0)
+        elif kind == "z":
+            ring.slow(k)
+        elif kind == "x":
+            ring.fast(k, j)
+        elif kind == "ys":
             ring.send_y(k, j)
-
-    def step(ring, k):
-        got = []
-        if k < A:
-            ring.slow(k)
-            got.append((k, 0))
-        for j in range(1, B):
-            ring.fast(k - 1, j)
-            got.append((k - 1, j))
-        waiting.extend((ring, *kj) for kj in got)
-        return got
-
-    gather()
-    before = []
-    for k in range(1, A + 1):
-        kept, waiting[:] = waiting[:], []
-        got = step(W, k)
-        pump(len(got))
-        waiting.extend(kept)
-        for kj in before:
-            W.relay(*kj)
-        before = got
-        step(Q, k)
-        if k < A:
-            pump(1)
-        if k == max(A - 1, 1):
-            load_o.wait()
-            O.slow(0)
-    pump(len(waiting))
-    for kj in before:
-        W.relay(*kj)
-    for kj in order:
-        W.from_core(*kj)
-    project_kv()
-    K.slow(0)
-    step(O, 1)
-    pump(len(waiting))
-    if A > 1:
-        K.slow(1)
-    for j in range(1, B):
-        K.fast(0, j)
-    if A > 1:
-        step(O, 2)
-        pump(len(waiting))
-    for kj in order:
-        Q.relay(*kj)
-    for kj in order:
-        Q.from_core(*kj)
-    project_q()
-    attend(seq, True)
-    for k in range(1, A):
-        if k + 1 < A:
-            K.slow(k + 1)
-        for j in range(1, B):
-            K.fast(k, j)
-        attend_past(k, 0)
-        for j in range(1, B):
-            attend_past(k - 1, j)
-        if k + 2 <= A:
-            step(O, k + 2)
-            pump(len(waiting))
-    for j in range(1, B):
-        attend_past(A - 1, j)
-    for kj in order:
-        O.relay(*kj)
-    for f in range(HEADS):
-        total = acc[f]
-        flip = (total[:HEAD_DIM] / total[HEAD_DIM : HEAD_DIM + 1]).T
-        att[:, f * HEAD_DIM : (f + 1) * HEAD_DIM] = flip.astype(BF16)
-
-    def project_out(s):
-        cols = pl.ds(pl.multiple_of(s * o_cols, o_cols), o_cols)
-        blk[:, cols] = jnp.dot(att[...], obuf[s], preferred_element_type=F32).astype(BF16)
-
-    if o_cols % 128 == 0:
-        project_out(seq)
-    for kj in order:
-        O.from_core(*kj)
-        if o_cols % 128 == 0:
-            project_out(piece_of(geo, *kj))
+        elif kind == "y":
+            ring.relay(k, j)
+        else:
+            ring.from_core(k, j)
     if o_cols % 128 != 0:
         for s in range(n):
             blk[:, s * o_cols : (s + 1) * o_cols] = jnp.dot(
@@ -462,16 +516,26 @@
         ring.finish()
 
 
-def add_kernel(tile, tok, ch, gates, oh, blk, out):
-    seq = lax.axis_index("seq")
-    t_rows = tile * pl.num_programs(0)
-    low = seq * t_rows + pl.program_id(0) * tile
-    rows = lax.broadcasted_iota(jnp.int32, (tile, 1), 0) + low
-    gate = jnp.sum(jnp.where(ch[...] == rows, gates[...], 0.0), axis=1, keepdims=True)
-    lift = lax.dot_general(
-        oh[...], blk[...], (((0,), (0,)), ((), ())), preferred_element_type=F32
-    )
-    out[...] = (tok[...].astype(F32) + gate * lift).astype(BF16)
+def add_kernel(tok, gate, oh, blk, out, made, sems):
+    tile = tok.shape[0] // ADD_TILES
+    copies = []
+    for i in range(ADD_TILES):
+        rows = pl.ds(i * tile, tile)
+        for first in range(0, tok.shape[1], 2 * HEAD_DIM):
+            right = blk[:, first : first + 2 * HEAD_DIM]
+            lift = jnp.dot(oh[rows, :], right, preferred_element_type=F32)
+            for j in range(0, 2 * HEAD_DIM, HEAD_DIM):
+                cols = slice(first + j, first + j + HEAD_DIM)
+                added = gate[rows, :] * lift[:, j : j + HEAD_DIM]
+                made[rows, cols] = (tok[rows, cols].astype(F32) + added).astype(BF16)
+        copies.append(pltpu.make_async_copy(made.at[rows], out.at[rows], sems.at[i]))
+        copies[-1].start()
+    for copy in copies:
+        copy.wait()
+
+
+def in_hbm(array):
+    return pltpu.with_memory_space_constraint(array, pltpu.HBM)
 
 
 def per_device(tokens, chosen, gates, w_query, w_key, w_value, w_out):
@@ -485,7 +549,7 @@
     picks = chosen.reshape(1, -1)
     gate_row = gates.reshape(1, -1)
     dma = pltpu.SemaphoreType.DMA
-    any_spec = pl.BlockSpec(memory_space=pl.ANY)
+    hbm_spec = pl.BlockSpec(memory_space=pltpu.HBM)
     vmem_spec = pl.BlockSpec(memory_space=pltpu.VMEM)
     steps_x = max(A * (B - 1), 1)
     steps_z = max(A - 1, 1)
@@ -496,7 +560,7 @@
     sems = []
     for _ in range(3):
         sems += [pair(steps_z), pair(steps_x), pair(n - 1), pair(2 * (n - 1))]
-    sems += [pair(KV_HEADS * steps_z), pair(KV_HEADS * steps_x)]
+    sems += [pair(KV_HEADS * steps_z), pair(KV_HEADS * steps_x), pair(KV_HEADS)]
     flat = [x for two in sems for x in two]
 
     def body(*refs):
@@ -504,15 +568,19 @@
         pairs = [(tail[i], tail[i + 1]) for i in range(0, len(tail), 2)]
         main_kernel(A, B, *head, *pairs)
 
-    blk, oh = pl.pallas_call(
+    blk, oh, gate = pl.pallas_call(
         body,
         out_shape=(
             jax.ShapeDtypeStruct((MOST_OWN, width), BF16),
-            jax.ShapeDtypeStruct((MOST_OWN, t_rows), BF16),
+            jax.ShapeDtypeStruct((t_rows, MOST_OWN), BF16),
+            jax.ShapeDtypeStruct((t_rows, HEAD_DIM), F32),
         ),
-        in_specs=[any_spec, vmem_spec] + [any_spec] * 4,
-        out_specs=(vmem_spec, vmem_spec),
+        in_specs=[hbm_spec] * 7,
+        out_specs=(vmem_spec, vmem_spec, vmem_spec),
         scratch_shapes=[
+            pltpu.VMEM(picks.shape, jnp.int32),
+            pltpu.VMEM(picks.shape, F32),
+            pltpu.VMEM((MOST_OWN, t_rows), F32),
             pltpu.VMEM((t_rows, width), BF16),
             pltpu.VMEM((n * k_rows, 2 * e_cols), BF16),
             pltpu.VMEM((n * k_rows, q_cols), BF16),
@@ -524,31 +592,26 @@
             pltpu.VMEM((HEADS, 1, MOST_OWN), F32),
             pltpu.VMEM((n, 1, HEAD_DIM), F32),
             pltpu.VMEM((MOST_OWN, HEADS * HEAD_DIM), BF16),
-            dma((2 * KV_HEADS + 3,)),
+            dma((2 * KV_HEADS + 5,)),
             *flat,
         ],
         compiler_params=pltpu.CompilerParams(
-            collective_id=0, has_side_effects=True, vmem_limit_bytes=60 * 1024 * 1024
+            collective_id=0, has_side_effects=True, vmem_limit_bytes=MAIN_VMEM * 1024 * 1024
         ),
         name="gather_attend",
-    )(tokens, picks, w_query, w_key, w_value, w_out)
-
-    tile = 256
+    )(
+        *map(in_hbm, (tokens, picks, gate_row, w_query, w_key, w_value, w_out))
+    )
+
     return pl.pallas_call(
-        functools.partial(add_kernel, tile),
-        grid=(t_rows // tile,),
+        add_kernel,
         out_shape=jax.ShapeDtypeStruct((t_rows, width), BF16),
-        in_specs=[
-            pl.BlockSpec((tile, width), lambda i: (i, 0)),
-            pl.BlockSpec(picks.shape, lambda i: (0, 0)),
-            pl.BlockSpec(picks.shape, lambda i: (0, 0)),
-            pl.BlockSpec((MOST_OWN, tile), lambda i: (0, i)),
-            pl.BlockSpec((MOST_OWN, width), lambda i: (0, 0)),
-        ],
-        out_specs=pl.BlockSpec((tile, width), lambda i: (i, 0)),
-        compiler_params=pltpu.CompilerParams(vmem_limit_bytes=62 * 1024 * 1024),
+        in_specs=[vmem_spec] * 4,
+        out_specs=hbm_spec,
+        scratch_shapes=[pltpu.VMEM((t_rows, width), BF16), dma((ADD_TILES,))],
+        compiler_params=pltpu.CompilerParams(vmem_limit_bytes=ADD_VMEM * 1024 * 1024),
         name="add_rows",
-    )(tokens, picks, gate_row, oh, blk)
+    )(tokens, gate, oh, blk)
 
 
 def solution(mesh):

time: 77.7 us -> 62.8 us (0.81)
  the two profiles are of different devices: /device:TPU:27 before, /device:TPU:0 now
where the time goes in v2:
time: 62.8 us; the launch traced here: 62.6 us
  Pallas kernels  62.5 us (100%)
    pallas_call x1, Pallas kernels, per_device(): pl.pallas_call(body, out_shape=(jax.ShapeDtypeStruct((MOST_OWN, width), B...  59.9 us
    pallas_call x1, Pallas kernels, per_device(): pl.pallas_call(add_kernel, out_shape=jax.ShapeDtypeStruct((t_rows, width)...  2.53 us

profile of v2, /device:TPU:0, one launch (start us, length us, event | category | flops | bytes accessed | tf_op | source)
XLA Modules:
  0.0 62.6 jit_solution(16935716454373662167)
XLA Ops:
  0.0 0.0 copy-start
  0.0 59.9 %gather_attend.1 = (bf16[256,2048]{1,0:T(8,128)(2,1)S(1)}, bf16[1024,256]{1,0:T(8,128)(2,1)S(1)}, f32[1024,128]{1,0:T(8,128)S(1)}) custom-call(bf16[1024,2048]{1,0:T(8,128)(2,1)} %tok.1, s32[1,1024]{1,0:T(1,128)} %bitcast.2, f32[1,1024]{1,0:T(1,128)} %bitcast.3, bf16[256,1024]{1,0:T(8,128)(2,1)} %refs_3_.1, bf16[256,256]{1,0:T(8,128)(2,1)} %refs_4_.1, ...), custom_call_target="tpu_custom_call" | custom-call | tf_op jit(solution)/shard_map/gather_attend/pallas_call | solution.py:571
  59.9 0.0 copy-done
  59.9 2.5 %add_rows.1 = bf16[1024,2048]{1,0:T(8,128)(2,1)} custom-call(bf16[1024,2048]{1,0:T(8,128)(2,1)S(1)} %copy-done, f32[1024,128]{1,0:T(8,128)S(1)} %get-tuple-element.8.gate, bf16[1024,256]{1,0:T(8,128)(2,1)S(1)} %get-tuple-element.9.oh, bf16[256,2048]{1,0:T(8,128)(2,1)S(1)} %get-tuple-element.10.blk), custom_call_target="tpu_custom_call" | custom-call | tf_op jit(solution)/shard_map/add_rows/pallas_call | solution.py:606
Async XLA Ops:
  0.0 59.9 %copy-start = (bf16[1024,2048]{1,0:T(8,128)(2,1)S(1)}, bf16[1024,2048]{1,0:T(8,128)(2,1)}, u32[]{:S(2)}) copy-start(bf16[1024,2048]{1,0:T(8,128)(2,1)} %tok.1) | copy-start | bytes 12582916

commit v3 on v2

--- a/solution.py
+++ b/solution.py
@@ -17,34 +17,35 @@
 MAIN_VMEM = 36
 ADD_VMEM = 12
 Q_SHARE = 9
-O_SHARE = 17
+O_SHARE = 18
 PLAN = (
-    ("W", "oz", 0, 0), ("Q", "ox", 0, 0), ("W", "ox", 0, 0), ("Q", "oz", 0, 0), ("gather",),
-    ("W", "z", 1, 0), ("W", "ys", 1, 0), ("O", "ox", 0, 0), ("gates", 0), ("Q", "x", 0, 1),
-    ("Q", "ys", 0, 1), ("Q", "z", 1, 0), ("gates", 1), ("Q", "ys", 1, 0), ("W", "x", 1, 1),
-    ("W", "z", 2, 0), ("gates", 2), ("W", "ys", 2, 0), ("O", "oz", 0, 0), ("W", "ys", 1, 1),
-    ("gates", 3), ("W", "x", 0, 1), ("W", "ys", 0, 1), ("W", "y", 1, 0), ("W", "z", 3, 0),
-    ("Q", "z", 2, 0), ("W", "ys", 3, 0), ("W", "x", 2, 1), ("W", "ys", 2, 1), ("Q", "y", 0, 1),
-    ("Q", "ys", 2, 0), ("W", "y", 0, 1), ("O", "x", 0, 1), ("O", "z", 1, 0), ("W", "x", 3, 1),
-    ("W", "y", 3, 0), ("Q", "x", 1, 1), ("W", "e", 0, 1), ("Q", "y", 1, 0), ("W", "ys", 3, 1),
-    ("Q", "z", 3, 0), ("W", "y", 2, 0), ("W", "y", 1, 1), ("Q", "ys", 1, 1), ("W", "y", 2, 1),
-    ("W", "e", 1, 0), ("W", "e", 3, 0), ("Q", "ys", 3, 0), ("Q", "x", 2, 1), ("O", "z", 2, 0),
-    ("W", "y", 3, 1), ("W", "e", 2, 1), ("O", "ys", 2, 0), ("W", "e", 2, 0), ("W", "e", 1, 1),
-    ("W", "e", 3, 1), ("kv",), ("K", "z", 0, 0, 1), ("Q", "x", 3, 1), ("K", "z", 0, 0, 0),
-    ("Q", "ys", 3, 1), ("Q", "ys", 2, 1), ("Q", "e", 0, 1), ("Q", "e", 1, 0), ("O", "z", 3, 0),
-    ("Q", "y", 1, 1), ("Q", "y", 2, 0), ("O", "ys", 1, 0), ("K", "z", 1, 0, 1), ("O", "x", 2, 1),
-    ("K", "z", 1, 0, 0), ("Q", "y", 2, 1), ("O", "ys", 0, 1), ("Q", "y", 3, 0), ("O", "ys", 3, 0),
-    ("O", "ys", 2, 1), ("K", "z", 2, 0, 1), ("Q", "y", 3, 1), ("O", "y", 2, 0), ("O", "x", 1, 1),
-    ("O", "x", 3, 1), ("Q", "e", 1, 1), ("Q", "e", 2, 0), ("Q", "e", 3, 0), ("Q", "e", 2, 1),
-    ("Q", "e", 3, 1), ("K", "z", 2, 0, 0), ("O", "y", 1, 0), ("q",), ("K", "x", 0, 1, 1),
-    ("O", "e", 2, 0), ("O", "y", 0, 1), ("O", "ys", 3, 1), ("O", "e", 1, 0), ("O", "ys", 1, 1),
-    ("K", "z", 3, 0, 1), ("K", "x", 0, 1, 0), ("own",), ("O", "e", 0, 1), ("att", 1, 0),
-    ("K", "x", 2, 1, 1), ("O", "y", 3, 0), ("K", "z", 3, 0, 0), ("att", 3, 0), ("att", 0, 1),
-    ("O", "y", 2, 1), ("K", "x", 3, 1, 1), ("att", 2, 0), ("K", "x", 2, 1, 0), ("att", 2, 1),
-    ("K", "x", 1, 1, 1), ("O", "y", 3, 1), ("O", "e", 3, 0), ("O", "e", 2, 1), ("K", "x", 3, 1, 0),
-    ("att", 3, 1), ("K", "x", 1, 1, 0), ("att", 1, 1), ("norm",), ("out", 0, 0), ("out", 2, 1),
-    ("O", "y", 1, 1), ("out", 3, 0), ("out", 0, 1), ("O", "e", 3, 1), ("out", 3, 1), ("out", 2, 0),
-    ("out", 1, 0), ("O", "e", 1, 1), ("out", 1, 1),
+    ("W", "oz", 0, 0), ("W", "ox", 0, 0), ("Q", "ox", 0, 0), ("Q", "oz", 0, 0), ("gather",),
+    ("W", "x", 0, 1), ("W", "ys", 0, 1), ("W", "z", 1, 0), ("W", "xe", 0, 0), ("W", "ys", 1, 0),
+    ("W", "z", 2, 0), ("O", "ox", 0, 0), ("W", "ys", 2, 0), ("O", "oz", 0, 0), ("Q", "x", 0, 1),
+    ("Q", "ys", 0, 1), ("W", "x", 1, 1), ("W", "ys", 1, 1), ("W", "z", 3, 0), ("gates", 0),
+    ("W", "ys", 3, 0), ("W", "y", 1, 0), ("gates", 2), ("Q", "z", 1, 0), ("W", "y", 2, 0),
+    ("W", "x", 2, 1), ("Q", "ys", 1, 0), ("W", "y", 0, 1), ("W", "ys", 2, 1), ("Q", "z", 2, 0),
+    ("W", "y", 1, 1), ("W", "e", 2, 0), ("W", "x", 3, 1), ("O", "z", 1, 0), ("W", "ys", 3, 1),
+    ("O", "z", 2, 0), ("O", "ys", 2, 0), ("Q", "x", 1, 1), ("Q", "ys", 2, 0), ("W", "y", 3, 0),
+    ("Q", "z", 3, 0), ("W", "e", 1, 1), ("W", "e", 1, 0), ("W", "e", 3, 0), ("Q", "ys", 1, 1),
+    ("W", "y", 2, 1), ("Q", "x", 2, 1), ("Q", "xe", 0, 0), ("W", "y", 3, 1), ("W", "e", 2, 1),
+    ("O", "z", 3, 0), ("Q", "y", 1, 0), ("W", "e", 3, 1), ("W", "e", 0, 1), ("kv",),
+    ("Q", "ys", 2, 1), ("K", "z", 0, 0, 1), ("O", "ys", 1, 0), ("K", "z", 0, 0, 0),
+    ("Q", "ys", 3, 0), ("O", "x", 0, 1), ("O", "y", 2, 0), ("Q", "y", 1, 1), ("O", "e", 2, 0),
+    ("Q", "x", 3, 1), ("Q", "y", 2, 0), ("Q", "ys", 3, 1), ("O", "x", 2, 1), ("O", "x", 1, 1),
+    ("K", "z", 1, 0, 1), ("Q", "e", 1, 1), ("gates", 1), ("K", "z", 1, 0, 0), ("O", "ys", 2, 1),
+    ("Q", "e", 2, 0), ("O", "ys", 3, 0), ("Q", "y", 3, 0), ("Q", "e", 1, 0), ("O", "ys", 0, 1),
+    ("Q", "y", 0, 1), ("O", "y", 1, 0), ("O", "ys", 1, 1), ("K", "x", 0, 1, 1), ("K", "z", 2, 0, 1),
+    ("Q", "e", 3, 0), ("O", "xe", 0, 0), ("O", "x", 3, 1), ("Q", "e", 0, 1), ("gates", 3),
+    ("O", "e", 1, 0), ("O", "ys", 3, 1), ("Q", "y", 2, 1), ("Q", "y", 3, 1), ("K", "z", 2, 0, 0),
+    ("Q", "e", 3, 1), ("Q", "e", 2, 1), ("K", "x", 0, 1, 0), ("q",), ("own",), ("O", "y", 2, 1),
+    ("K", "z", 3, 0, 1), ("att", 0, 1), ("att", 2, 0), ("K", "x", 1, 1, 1), ("K", "z", 3, 0, 0),
+    ("O", "y", 0, 1), ("O", "y", 3, 0), ("att", 3, 0), ("att", 1, 0), ("K", "x", 1, 1, 0),
+    ("O", "y", 1, 1), ("O", "e", 2, 1), ("O", "e", 0, 1), ("O", "e", 3, 0), ("K", "x", 3, 1, 1),
+    ("K", "x", 2, 1, 1), ("att", 1, 1), ("K", "x", 2, 1, 0), ("O", "e", 1, 1), ("att", 2, 1),
+    ("O", "y", 3, 1), ("K", "x", 3, 1, 0), ("att", 3, 1), ("norm",), ("out", 0, 0), ("out", 3, 0),
+    ("out", 0, 1), ("out", 2, 1), ("O", "e", 3, 1), ("out", 1, 0), ("out", 3, 1), ("out", 2, 0),
+    ("out", 1, 1),
 )
 MESH = pl.DeviceIdType.MESH
 NEG = -1e30
@@ -59,15 +60,18 @@
         self.region_in = region_in
         self.region_y = region_y
         self.sends = []
+        self.some = []
+        self.whole = geo["B"] == 2
         a_count, b_count = geo["A"], geo["B"]
         self.order = arrivals(a_count, b_count)
 
     def piece(self, k, j):
-        return piece_of(self.g, k, j)
+        g = self.g
+        b = lax.rem(g["b"] - j + g["B"], g["B"])
+        return at_row(g, lambda row: by_distance(g["A"], row)[k]) * g["B"] + b
 
     def copy(self, kind, index, ref, dp, seq):
-        send, recv = self.sems[kind]
-        return remote(ref, send.at[index], recv.at[index], dp, seq)
+        return remote(ref, self.sems["sent"].at[0], self.sems[kind].at[index], dp, seq)
 
     def send(self, *args):
         made = self.copy(*args)
@@ -75,7 +79,7 @@
         self.sends.append(made)
 
     def arrive(self, kind, index, ref):
-        self.copy(kind, index, ref, self.g["dp"], self.g["z_next"]).wait_recv()
+        self.copy(kind, index, ref, self.g["dp"], self.g["x_next"]).wait_recv()
 
     def mine(self, s):
         return self.region_in(s, self.g["y"], self.g["c"])
@@ -87,12 +91,46 @@
     def send_y(self, k, j):
         g = self.g
         ref = self.region_y(self.piece(k, j), g["y"], g["c"])
-        self.send("y", self.order.index((k, j)), ref, g["dp_y"], g["seq"])
-
-    def send_z(self, k):
-        g = self.g
-        if k < g["A"] - 1:
-            self.send("z", k, self.mine(self.piece(k, 0)), g["dp"], g["z_next"])
+        args = ("y", self.order.index((k, j)), ref, g["dp_y"], g["seq"])
+        if self.whole and (k, j) == (0, 1):
+            self.send_if(g["a"] > 0, *args)
+        else:
+            self.send(*args)
+
+    def send_rest(self):
+        g = self.g
+        if self.whole:
+            ref = self.region_y(self.piece(0, 0), 1 - g["y"], g["c"])
+            self.send_if(g["a"] == 0, "r", 0, ref, g["dp"], g["x_next"])
+
+    def send_if(self, cond, *args):
+        made = self.copy(*args)
+        pl.when(cond)(made.start)
+        self.some.append((cond, made))
+
+    def send_z(self):
+        g = self.g
+        mine = self.mine(self.piece(0, 0))
+        self.send_if(g["a"] < g["A"] - 1, "u", 0, mine, g["dp"], g["z_up"])
+        self.send_if(g["a"] > 0, "v", 0, mine, g["dp"], g["z_down"])
+
+    def take_z(self, k):
+        g = self.g
+        mine = self.mine(self.piece(k, 0))
+        for far in range(1, g["A"]):
+            for kind, sign, to in (("u", -1, g["z_up"]), ("v", 1, g["z_down"])):
+                rows = [
+                    row
+                    for row in range(g["A"])
+                    if by_distance(g["A"], row)[k] == row + sign * far
+                ]
+                if not rows:
+                    continue
+                here = any_row(g, rows)
+                pl.when(here)(self.copy(kind, far - 1, mine, g["dp"], to).wait_recv)
+                onward = [row for row in rows if 0 <= row - sign < g["A"]]
+                if onward:
+                    self.send_if(any_row(g, onward), kind, far, mine, g["dp"], to)
 
     def send_x(self, k):
         g = self.g
@@ -101,8 +139,7 @@
             self.send("x", k * (g["B"] - 1), ref, g["dp"], g["x_next"])
 
     def slow(self, k):
-        self.arrive("z", k - 1, self.mine(self.piece(k, 0)))
-        self.send_z(k)
+        self.take_z(k)
         self.send_x(k)
         self.send_core(k, 0)
 
@@ -118,7 +155,13 @@
         g = self.g
         index = self.order.index((k, j))
         ref = self.region_y(self.piece(k, j), 1 - g["y"], g["c"])
-        self.arrive("y", index, ref)
+        if self.whole and (k, j) == (0, 1):
+            rest = self.copy("r", 0, ref, g["dp"], g["x_next"])
+            over = self.copy("y", index, ref, g["dp_y"], g["seq"])
+            pl.when(g["a"] == 0)(rest.wait_recv)
+            pl.when(g["a"] > 0)(over.wait_recv)
+        else:
+            self.arrive("y", index, ref)
         self.send("d", len(self.order) + index, ref, g["dp_c"], g["seq"])
 
     def from_core(self, k, j):
@@ -131,6 +174,8 @@
     def finish(self):
         for made in self.sends:
             made.wait_send()
+        for cond, made in self.some:
+            pl.when(cond)(made.wait_send)
 
 
 class Causal:
@@ -150,9 +195,8 @@
         return g["b"] >= j
 
     def copy(self, kind, index, e, s, seq):
-        send, recv = self.sems[kind]
-        at = index * self.parts + e
-        return remote(self.ref(s, e), send.at[at], recv.at[at], self.g["dp"], seq)
+        recv = self.sems[kind].at[index * self.parts + e]
+        return remote(self.ref(s, e), self.sems["sent"].at[0], recv, self.g["dp"], seq)
 
     def send(self, cond, *args):
         made = self.copy(*args)
@@ -160,7 +204,7 @@
         self.sends.append((cond, made))
 
     def arrive(self, cond, *args):
-        pl.when(cond)(self.copy(*args, self.g["z_next"]).wait_recv)
+        pl.when(cond)(self.copy(*args, self.g["z_up"]).wait_recv)
 
     def slow(self, k, e):
         g = self.g
@@ -169,7 +213,7 @@
             self.arrive(g["a"] >= k, "z", k - 1, e, s)
         if k < g["A"] - 1:
             cond = jnp.logical_and(g["a"] >= k, g["a"] + 1 < g["A"])
-            self.send(cond, "z", k, e, s, g["z_next"])
+            self.send(cond, "z", k, e, s, g["z_up"])
         if g["B"] > 1:
             cond = g["a"] >= k if k > 0 else g["b"] + 1 < g["B"]
             if self.detour and k == 1:
@@ -189,7 +233,7 @@
         self.arrive(has, "x", index, e, s)
         if self.detour and k == 0:
             cond = jnp.logical_and(g["a"] == g["A"] - 2, g["b"] == 1)
-            self.send(cond, "t", 0, e, s, g["z_next"])
+            self.send(cond, "t", 0, e, s, g["z_up"])
         if j < g["B"] - 1:
             cond = self.has(k, j)
             if k == 0:
@@ -219,6 +263,24 @@
     return order + [(a_count - 1, j) for j in range(1, b_count)]
 
 
+def by_distance(count, row):
+    return sorted(range(count), key=lambda other: (abs(other - row), other))
+
+
+def at_row(g, value):
+    result = value(0)
+    for row in range(1, g["A"]):
+        result = jnp.where(g["a"] == row, value(row), result)
+    return result
+
+
+def any_row(g, rows):
+    result = g["a"] == rows[0]
+    for row in rows[1:]:
+        result = jnp.logical_or(result, g["a"] == row)
+    return result
+
+
 def piece_of(g, k, j):
     a = lax.rem(g["a"] - k + g["A"], g["A"])
     b = lax.rem(g["b"] - j + g["B"], g["B"])
@@ -231,24 +293,33 @@
     order = arrivals(A, B)
     taken = {kj: ("z" if kj[1] == 0 else "x", *kj) for kj in order}
     parts = range(KV_HEADS)
-    plan = [("W", "oz", 0, 0), ("W", "ox", 0, 0), ("Q", "oz", 0, 0), ("Q", "ox", 0, 0), ("gather",)]
+    plan = [("gather",)]
+    for what in "WQ":
+        plan += [(what, "oz", 0, 0), (what, "ox", 0, 0)]
     for what in "WQ":
         for kj in order:
             plan += [(what, *taken[kj]), (what, "ys", *kj)]
-    plan += [("O", "oz", 0, 0), ("O", "ox", 0, 0)]
+    for what in "O":
+        plan += [(what, "oz", 0, 0), (what, "ox", 0, 0)]
     plan += [("W", "y", *kj) for kj in order] + [("W", "e", *kj) for kj in order]
-    plan += [("gates", i) for i in range(TILES)] + [("kv",)] + [("K", "z", 0, 0, e) for e in parts]
+    plan += [("gates", i) for i in range(TILES)] + [("kv",)]
+    plan += [("K", "z", 0, 0, e) for e in parts]
     for kj in order[: len(order) // 2]:
-        plan += [("O", *taken[kj]), ("O", "ys", *kj)]
-    plan += [("Q", "y", *kj) for kj in order] + [("Q", "e", *kj) for kj in order]
+        for what in "O":
+            plan += [(what, *taken[kj]), (what, "ys", *kj)]
+    for what in "Q":
+        plan += [(what, "y", *kj) for kj in order] + [(what, "e", *kj) for kj in order]
     plan += [("q",), ("own",)]
     for i, kj in enumerate(order):
         plan += [("K", *taken[kj], e) for e in parts] + [("att", *kj)]
         if i >= len(order) // 2:
-            plan += [("O", *taken[kj]), ("O", "ys", *kj)]
-    plan += [("O", "y", *kj) for kj in order] + [("norm",), ("out", 0, 0)]
+            for what in "O":
+                plan += [(what, *taken[kj]), (what, "ys", *kj)]
+    for what in "O":
+        plan += [(what, "y", *kj) for kj in order]
+    plan += [("norm",), ("out", 0, 0)]
     for kj in order:
-        plan += [("O", "e", *kj), ("out", *kj)]
+        plan += [(what, "e", *kj) for what in "O"] + [("out", *kj)]
     return plan
 
 
@@ -259,22 +330,22 @@
 def main_kernel(
     A, B, tok, ch_in, gates_in, wq, wk, wv, wo, blk, oh_out, gate_out,
     ch, gates, oh, tok_v, kvw, qw, obuf, kv, normed, qt, acc, m_s, counts, att, lsem,
-    wz, wx, wy, wd, qz, qx, qy, qd, oz, ox, oy, od, kz, kx, kt,
+    sent, *sems,
 ):
     n = A * B
     dp = lax.axis_index("dp")
     seq = lax.axis_index("seq")
     a, b = seq // B, lax.rem(seq, B)
     y, c = lax.rem(dp // 2, 2), lax.rem(dp, 2)
-    z_next = lax.rem(a + 1, A) * B + b
-    z_prev = lax.rem(a + A - 1, A) * B + b
+    z_up = lax.rem(a + 1, A) * B + b
+    z_down = lax.rem(a + A - 1, A) * B + b
     x_next = a * B + lax.rem(b + 1, B)
     x_prev = a * B + lax.rem(b + B - 1, B)
     dp_y = dp + 2 * (1 - 2 * y)
     dp_c = dp + 1 - 2 * c
     geo = dict(
         A=A, B=B, a=a, b=b, y=y, c=c, dp=dp, seq=seq,
-        z_next=z_next, x_next=x_next, dp_y=dp_y, dp_c=dp_c,
+        z_up=z_up, z_down=z_down, x_next=x_next, dp_y=dp_y, dp_c=dp_c,
     )
     t_rows = tok.shape[0]
     width = tok.shape[1]
@@ -298,14 +369,24 @@
     load_kv, rest = local[: 2 * KV_HEADS], local[2 * KV_HEADS :]
     load_q, load_ch, load_tok, load_o, load_gates = rest
 
-    greet = [(dp, z_next)] + ([(dp, z_prev)] if A > 2 else [])
+    greet = [(dp_y, seq), (dp_c, seq)]
     if B > 1:
         greet += [(dp, x_next)] + ([(dp, x_prev)] if B > 2 else [])
-    greet += [(dp_y, seq), (dp_c, seq)]
     barrier = pltpu.get_barrier_semaphore()
+
+    def hail(who):
+        pl.semaphore_signal(barrier, inc=1, device_id=who, device_id_type=MESH)
+
     for who in greet:
-        pl.semaphore_signal(barrier, inc=1, device_id=who, device_id_type=MESH)
-    pl.semaphore_wait(barrier, len(greet))
+        hail(who)
+    if A > 1:
+        inner = jnp.logical_and(a > 0, a < A - 1)
+        pl.when(a < A - 1)(lambda: hail((dp, z_up)))
+        pl.when(a > 0)(lambda: hail((dp, z_down)))
+        pl.when(inner)(lambda: pl.semaphore_wait(barrier, len(greet) + 2))
+        pl.when(jnp.logical_not(inner))(lambda: pl.semaphore_wait(barrier, len(greet) + 1))
+    else:
+        pl.semaphore_wait(barrier, len(greet))
 
     quarter = 2 * e_cols // 4
 
@@ -330,23 +411,26 @@
     def o_region(s, start, size):
         return obuf.at[s, pl.ds(pl.multiple_of(start, 16), size), :]
 
-    W = Ring(geo, {"z": wz, "x": wx, "y": wy, "d": wd}, w_region, w_region)
+    w_sems, q_sems, o_sems = (
+        dict(zip("uvxydr", sems[6 * i : 6 * i + 6]), sent=sent) for i in range(3)
+    )
+    kz, kx, kt = sems[18:]
+    W = Ring(geo, w_sems, w_region, w_region)
     Q = Ring(
         geo,
-        {"z": qz, "x": qx, "y": qy, "d": qd},
+        q_sems,
         lambda s, y, c: q_region(s, c, y * (k_rows - q_in), q_in),
         lambda s, y, c: q_region(s, c, y * q_in, k_rows - q_in),
     )
     O = Ring(
         geo,
-        {"z": oz, "x": ox, "y": oy, "d": od},
+        o_sems,
         lambda s, y, c: o_region(s, c * o_half + y * (o_half - o_in), o_in),
         lambda s, y, c: o_region(s, c * o_half + y * o_in, o_half - o_in),
     )
-    K = Causal(geo, {"z": kz, "x": kx, "t": kt}, lambda s, e: kv.at[s, e], KV_HEADS)
-
     rings = {"W": W, "Q": Q, "O": O}
     loads = {"W": load_kv, "Q": [load_q], "O": [load_o]}
+    K = Causal(geo, {"z": kz, "x": kx, "t": kt, "sent": sent}, lambda s, e: kv.at[s, e], KV_HEADS)
 
     def gather():
         load_ch.wait()
@@ -460,7 +544,7 @@
 
     def project_out(k, j):
         if o_cols % 128 == 0:
-            s = piece_of(geo, k, j)
+            s = W.piece(k, j)
             cols = pl.ds(pl.multiple_of(s * o_cols, o_cols), o_cols)
             blk[:, cols] = jnp.dot(
                 att[...], obuf[s], preferred_element_type=F32
@@ -489,14 +573,16 @@
             continue
         ring = rings[what]
         kind, k, j = at
-        if kind in ("oz", "ox"):
+        if kind in ("oz", "ox", "xe"):
             for made in loads[what]:
                 made.wait()
             loads[what] = []
         if kind == "oz":
-            ring.send_z(0)
+            ring.send_z()
         elif kind == "ox":
             ring.send_x(0)
+        elif kind == "xe":
+            ring.send_rest()
         elif kind == "z":
             ring.slow(k)
         elif kind == "x":
@@ -512,7 +598,7 @@
             blk[:, s * o_cols : (s + 1) * o_cols] = jnp.dot(
                 att[...], obuf[s], preferred_element_type=F32
             ).astype(BF16)
-    for ring in (W, Q, O, K):
+    for ring in (*rings.values(), K):
         ring.finish()
 
 
@@ -554,19 +640,12 @@
     steps_x = max(A * (B - 1), 1)
     steps_z = max(A - 1, 1)
 
-    def pair(count):
-        return (dma((count,)), dma((count,)))
-
-    sems = []
-    for _ in range(3):
-        sems += [pair(steps_z), pair(steps_x), pair(n - 1), pair(2 * (n - 1))]
-    sems += [pair(KV_HEADS * steps_z), pair(KV_HEADS * steps_x), pair(KV_HEADS)]
-    flat = [x for two in sems for x in two]
+    counts = [steps_z, steps_z, steps_x, n - 1, 2 * (n - 1), 1] * 3
+    counts += [KV_HEADS * steps_z, KV_HEADS * steps_x, KV_HEADS]
+    flat = [dma((1,))] + [dma((count,)) for count in counts]
 
     def body(*refs):
-        head, tail = refs[: len(refs) - len(flat)], refs[len(refs) - len(flat) :]
-        pairs = [(tail[i], tail[i + 1]) for i in range(0, len(tail), 2)]
-        main_kernel(A, B, *head, *pairs)
+        main_kernel(A, B, *refs)
 
     blk, oh, gate = pl.pallas_call(
         body,

time: 62.8 us -> 59.8 us (0.952)
  the two profiles are of different devices: /device:TPU:0 before, /device:TPU:27 now
where the time goes in v3:
time: 59.8 us; the launch traced here: 59.2 us
  Pallas kernels  59 us (99%)
    pallas_call x1, Pallas kernels, per_device(): pl.pallas_call(body, out_shape=(jax.ShapeDtypeStruct((MOST_OWN, width), B...  56.5 us
    pallas_call x1, Pallas kernels, per_device(): pl.pallas_call(add_kernel, out_shape=jax.ShapeDtypeStruct((t_rows, width)...  2.53 us

profile of v3, /device:TPU:27, one launch (start us, length us, event | category | flops | bytes accessed | tf_op | source)
XLA Modules:
  0.0 59.2 jit_solution(1189148353698432072)
XLA Ops:
  0.0 0.0 copy-start
  0.0 56.5 %gather_attend.1 = (bf16[256,2048]{1,0:T(8,128)(2,1)S(1)}, bf16[1024,256]{1,0:T(8,128)(2,1)S(1)}, f32[1024,128]{1,0:T(8,128)S(1)}) custom-call(bf16[1024,2048]{1,0:T(8,128)(2,1)} %tok.1, s32[1,1024]{1,0:T(1,128)} %bitcast.2, f32[1,1024]{1,0:T(1,128)} %bitcast.3, bf16[256,1024]{1,0:T(8,128)(2,1)} %refs_3_.1, bf16[256,256]{1,0:T(8,128)(2,1)} %refs_4_.1, ...), custom_call_target="tpu_custom_call" | custom-call | tf_op jit(solution)/shard_map/gather_attend/pallas_call | solution.py:650
  56.5 0.0 copy-done
  56.5 2.5 %add_rows.1 = bf16[1024,2048]{1,0:T(8,128)(2,1)} custom-call(bf16[1024,2048]{1,0:T(8,128)(2,1)S(1)} %copy-done, f32[1024,128]{1,0:T(8,128)S(1)} %get-tuple-element.8.gate, bf16[1024,256]{1,0:T(8,128)(2,1)S(1)} %get-tuple-element.9.oh, bf16[256,2048]{1,0:T(8,128)(2,1)S(1)} %get-tuple-element.10.blk), custom_call_target="tpu_custom_call" | custom-call | tf_op jit(solution)/shard_map/add_rows/pallas_call | solution.py:685
Async XLA Ops:
  0.0 56.5 %copy-start = (bf16[1024,2048]{1,0:T(8,128)(2,1)S(1)}, bf16[1024,2048]{1,0:T(8,128)(2,1)}, u32[]{:S(2)}) copy-start(bf16[1024,2048]{1,0:T(8,128)(2,1)} %tok.1) | copy-start | bytes 12582916

commit v4 on v3

--- a/solution.py
+++ b/solution.py
@@ -54,13 +54,16 @@
 
 
 class Ring:
-    def __init__(self, geo, sems, region_in, region_y):
+    def __init__(self, geo, sems, region_in, region_y, taken, each=False):
         self.g = geo
         self.sems = sems
         self.region_in = region_in
         self.region_y = region_y
         self.sends = []
         self.some = []
+        self.taken = taken
+        self.asked = 0
+        self.each = each
         self.whole = geo["B"] == 2
         a_count, b_count = geo["A"], geo["B"]
         self.order = arrivals(a_count, b_count)
@@ -84,9 +87,12 @@
     def mine(self, s):
         return self.region_in(s, self.g["y"], self.g["c"])
 
+    def core_at(self, k, j):
+        return self.order.index((k, j)) if self.each else 0
+
     def send_core(self, k, j):
         g = self.g
-        self.send("d", self.order.index((k, j)), self.mine(self.piece(k, j)), g["dp_c"], g["seq"])
+        self.send("d", self.core_at(k, j), self.mine(self.piece(k, j)), g["dp_c"], g["seq"])
 
     def send_y(self, k, j):
         g = self.g
@@ -162,14 +168,16 @@
             pl.when(g["a"] > 0)(over.wait_recv)
         else:
             self.arrive("y", index, ref)
-        self.send("d", len(self.order) + index, ref, g["dp_c"], g["seq"])
+        self.send("d", self.core_at(k, j), ref, g["dp_c"], g["seq"])
 
     def from_core(self, k, j):
         g = self.g
-        index = self.order.index((k, j))
-        s = self.piece(k, j)
-        self.arrive("d", index, self.region_in(s, g["y"], 1 - g["c"]))
-        self.arrive("d", len(self.order) + index, self.region_y(s, 1 - g["y"], 1 - g["c"]))
+        if self.each:
+            self.arrive("d", self.core_at(k, j), self.taken(self.piece(k, j), 1 - g["c"]))
+            return
+        self.asked += 1
+        if self.asked == len(self.order):
+            self.arrive("d", 0, self.taken)
 
     def finish(self):
         for made in self.sends:
@@ -415,18 +423,22 @@
         dict(zip("uvxydr", sems[6 * i : 6 * i + 6]), sent=sent) for i in range(3)
     )
     kz, kx, kt = sems[18:]
-    W = Ring(geo, w_sems, w_region, w_region)
+    others = pl.ds(0, (n - 1) * k_rows)
+    W = Ring(geo, w_sems, w_region, w_region, kvw.at[others, pl.ds(0, 2 * quarter)])
     Q = Ring(
         geo,
         q_sems,
         lambda s, y, c: q_region(s, c, y * (k_rows - q_in), q_in),
         lambda s, y, c: q_region(s, c, y * q_in, k_rows - q_in),
+        qw.at[others, pl.ds(0, q_half)],
     )
     O = Ring(
         geo,
         o_sems,
         lambda s, y, c: o_region(s, c * o_half + y * (o_half - o_in), o_in),
         lambda s, y, c: o_region(s, c * o_half + y * o_in, o_half - o_in),
+        lambda s, c: o_region(s, c * o_half, o_half),
+        each=True,
     )
     rings = {"W": W, "Q": Q, "O": O}
     loads = {"W": load_kv, "Q": [load_q], "O": [load_o]}
@@ -640,7 +652,9 @@
     steps_x = max(A * (B - 1), 1)
     steps_z = max(A - 1, 1)
 
-    counts = [steps_z, steps_z, steps_x, n - 1, 2 * (n - 1), 1] * 3
+    counts = []
+    for cores in (1, 1, n - 1):
+        counts += [steps_z, steps_z, steps_x, n - 1, cores, 1]
     counts += [KV_HEADS * steps_z, KV_HEADS * steps_x, KV_HEADS]
     flat = [dma((1,))] + [dma((count,)) for count in counts]
 

time: 59.8 us -> 59 us (0.987)
  Pallas kernels: 59 us -> 58 us
    pallas_call x1, Pallas kernels: 56.5 us -> 55.5 us  [per_device(): pl.pallas_call(body, out_shape=(jax.ShapeDtypeStruct((MOST_OWN, width), B...]
where the time goes in v4:
time: 59 us; the launch traced here: 58.2 us
  Pallas kernels  58 us (98%)
    pallas_call x1, Pallas kernels, per_device(): pl.pallas_call(body, out_shape=(jax.ShapeDtypeStruct((MOST_OWN, width), B...  55.5 us
    pallas_call x1, Pallas kernels, per_device(): pl.pallas_call(add_kernel, out_shape=jax.ShapeDtypeStruct((t_rows, width)...  2.53 us

profile of v4, /device:TPU:27, one launch (start us, length us, event | category | flops | bytes accessed | tf_op | source)
XLA Modules:
  0.0 58.2 jit_solution(10433238681100637991)
XLA Ops:
  0.0 0.0 copy-start
  0.0 55.5 %gather_attend.1 = (bf16[256,2048]{1,0:T(8,128)(2,1)S(1)}, bf16[1024,256]{1,0:T(8,128)(2,1)S(1)}, f32[1024,128]{1,0:T(8,128)S(1)}) custom-call(bf16[1024,2048]{1,0:T(8,128)(2,1)} %tok.1, s32[1,1024]{1,0:T(1,128)} %bitcast.2, f32[1,1024]{1,0:T(1,128)} %bitcast.3, bf16[256,1024]{1,0:T(8,128)(2,1)} %refs_3_.1, bf16[256,256]{1,0:T(8,128)(2,1)} %refs_4_.1, ...), custom_call_target="tpu_custom_call" | custom-call | tf_op jit(solution)/shard_map/gather_attend/pallas_call | solution.py:664
  55.5 0.0 copy-done
  55.5 2.5 %add_rows.1 = bf16[1024,2048]{1,0:T(8,128)(2,1)} custom-call(bf16[1024,2048]{1,0:T(8,128)(2,1)S(1)} %copy-done, f32[1024,128]{1,0:T(8,128)S(1)} %get-tuple-element.8.gate, bf16[1024,256]{1,0:T(8,128)(2,1)S(1)} %get-tuple-element.9.oh, bf16[256,2048]{1,0:T(8,128)(2,1)S(1)} %get-tuple-element.10.blk), custom_call_target="tpu_custom_call" | custom-call | tf_op jit(solution)/shard_map/add_rows/pallas_call | solution.py:699
Async XLA Ops:
  0.0 55.5 %copy-start = (bf16[1024,2048]{1,0:T(8,128)(2,1)S(1)}, bf16[1024,2048]{1,0:T(8,128)(2,1)}, u32[]{:S(2)}) copy-start(bf16[1024,2048]{1,0:T(8,128)(2,1)} %tok.1) | copy-start | bytes 12582916
